TPU v7x, 512 devices: a whole 4x4x16 slice. The times are simulated.
512 devices in a mesh: seq: 8 (over y_hi, x), col: 16 (over z), head: 4 (over y_lo, core).
Axes of the slice: x: 4, y: 4 (y_hi: 2, y_lo: 2; y = y_hi * 2 + y_lo), z: 16, core: 2. Of those that a mesh axis runs over, the one named last changes fastest.
Arguments:
- sequence_matrix: bfloat16 [128, 512, 256], P('seq', 'col'), may hold values from -24 to 24
- sequence_presence: int32 [128, 512], P('seq', 'col'), may hold values 0 or 1
- couple_matrix: bfloat16 [512, 512, 128], P('seq', 'col'), may hold values from -6 to 6
- couple_delta_selector: int32 [512, 512], P('seq', 'col'), may hold values 0 or 1
- softmax_scaling_vector: float32 [256], replicated, may hold values from 0.1 to 1.9
- couple_scaling_vector: float32 [128], replicated, may hold values from 0.1 to 1.9
- couple_logit_matrix: bfloat16 [128, 8], P(None, 'head'), may hold values from -44 to 44
- query_value_matrices: bfloat16 [256, 8, 128], P(None, 'head'), may hold values from -0.375 to 0.375
- merging_matrix: bfloat16 [256, 256], P('head'), may hold values from -0.375 to 0.375
- tensor_average_scaling: float32 [256], replicated, may hold values from 0.1 to 1.9
- factor_mapping_matrix: bfloat16 [256, 64], replicated, may hold values from -0.375 to 0.375
- tensor_average_matrix: bfloat16 [1024, 128], replicated, may hold values from -0.1875 to 0.1875
Outputs:
- sequence_refreshed: bfloat16 [128, 512, 256], P('seq', 'col')
- pair_output: bfloat16 [512, 512, 128], P('seq', 'col')
All inputs are finite; a program needn't handle non-finite values. No bound on the sum of `sequence_presence` or of `couple_delta_selector` on one device may be relied on, other than what follows from the above.
Results may differ from a plain program's by a relative error of at most 0.005.
The roundings to bfloat16 on the way count: a program that leaves them out, or rounds other values in their place, can miss the bound.
Values may be sent and summed in bfloat16 or wider, within the bound.
No kernel may reach another device: no remote copies, remote signals or barrier semaphores. Data moves between devices by JAX's collectives and lax.ppermute only.
A program may use at most 64 MiB of HBM per device.

v0:
```python
import math

import jax
import jax.numpy as jnp
from jax import lax
from jax.sharding import Mesh
from jax.sharding import PartitionSpec as P

SEQ = ("seq_0", "seq_1")
SEQ_COL = ("seq_0", "seq_1", "col")


EPSILON = 1e-05
MASKED_FILL = -1000000000.0


def laid_out(tiles, dim):
    tiles = jnp.moveaxis(tiles, 0, dim)
    dims = tiles.shape
    return tiles.reshape(*dims[:dim], dims[dim] * dims[dim + 1], *dims[dim + 2 :])


def gather_in_order(value, axes, order):
    tiles = value
    for k in order:
        tiles = lax.all_gather(tiles, axes[k])
    done = order[::-1]
    back = [done.index(k) for k in range(len(axes))]
    tiles = tiles.transpose(*back, *range(len(axes), tiles.ndim))
    return tiles.reshape(-1, *value.shape)


def gathered_by_axis(value, axes, order, dim):
    return laid_out(gather_in_order(value, axes, order), dim)


def in_one_piece(arrays, axis, split_dim, concat_dim, along):
    columns = [a.reshape(*a.shape[:along], -1) for a in arrays]
    both = jnp.concatenate(columns, axis=along)
    whole, at, finished = (
        lax.all_to_all(both, axis, split_axis=split_dim, concat_axis=concat_dim, tiled=True),
        0,
        [],
    )
    for a, column in zip(arrays, columns):
        section = whole[..., at : at + column.shape[along]]
        finished.append(section.reshape(*section.shape[:along], *a.shape[along:]))
        at += column.shape[along]
    return tuple(finished)


def gather_packed(arrays, axis, dims):
    vector = jnp.concatenate([a.reshape(-1) for a in arrays])
    lines, at, finished = (lax.all_gather(vector, axis), 0, [])
    for a, dim in zip(arrays, dims):
        tiles = lines[:, at : at + a.size].reshape(-1, *a.shape)
        finished.append(laid_out(tiles, dim))
        at += a.size
    return tuple(finished)


def in_one_piece_2(arrays, axis, dim, along):
    widths = [math.prod(a.shape[along:]) for a in arrays]
    both = jnp.concatenate(
        [a.reshape(*a.shape[:along], w) for a, w in zip(arrays, widths)], axis=along
    )
    whole = lax.all_gather(both, axis, axis=dim, tiled=True)
    tiles = jnp.split(whole, [sum(widths[:k]) for k in range(1, len(widths))], axis=along)
    return tuple((b.reshape(*whole.shape[:along], *a.shape[along:]) for a, b in zip(arrays, tiles)))


def sent_together(arrays, axis, dim, along):
    ends, at = ([], 0)
    for a in arrays[:-1]:
        at += a.shape[along]
        ends.append(at)
    both = jnp.concatenate(arrays, axis=along)
    return tuple(jnp.split(lax.all_gather(both, axis, axis=dim, tiled=True), ends, axis=along))


def copy_for_each(value, axis):
    length = lax.axis_size(axis)
    return lax.all_to_all(
        jnp.broadcast_to(value[None], (length, *value.shape)), axis, 0, 0, tiled=True
    )


def collect(value, axis, dim):
    return laid_out(copy_for_each(value, axis), dim)


def standardize_features(input_arrays, gain_vec):
    values_f = input_arrays.astype(jnp.float32)
    average = jnp.mean(values_f, axis=-1, keepdims=True)
    centered = values_f - average
    variance = jnp.mean(centered * centered, axis=-1, keepdims=True)
    return centered * lax.rsqrt(variance + EPSILON) * gain_vec


def local(
    sequence_matrix,
    sequence_presence,
    couple_matrix,
    couple_delta_selector,
    softmax_scaling_vector,
    couple_scaling_vector,
    couple_logit_matrix,
    query_value_matrices,
    merging_matrix,
    tensor_average_scaling,
    factor_mapping_matrix,
    tensor_average_matrix,
):
    local_sequence_total, local_position_total, feature_number = sequence_matrix.shape
    tile_rows, tile_cols, pair_width = couple_matrix.shape
    heads_here = couple_logit_matrix.shape[1]
    head_dim = query_value_matrices.shape[2] // 4
    seq_count = lax.axis_size(SEQ)
    col_count = lax.axis_size("col")
    score_scale = head_dim ** (-0.5)
    pair_normed = standardize_features(couple_matrix, couple_scaling_vector).astype(jnp.bfloat16)
    tile_bias = jnp.dot(
        pair_normed.reshape(tile_rows * tile_cols, pair_width),
        couple_logit_matrix,
        preferred_element_type=jnp.float32,
    )
    tile_bias = (
        tile_bias.astype(jnp.bfloat16)
        .reshape(tile_rows, tile_cols, heads_here)
        .transpose(2, 0, 1)[None]
    )
    gathered_tiles = gathered_by_axis(tile_bias, SEQ_COL, (0, 1, 2), 0)
    bias_plane = gathered_tiles.reshape(seq_count, col_count, heads_here, tile_rows, tile_cols)
    bias_plane = bias_plane.transpose(2, 0, 3, 1, 4).reshape(
        heads_here, seq_count * tile_rows, col_count * tile_cols
    )
    plane_float = bias_plane.astype(jnp.float32)
    sequence_standardized = standardize_features(sequence_matrix, softmax_scaling_vector).astype(
        jnp.bfloat16
    )
    linear_mapped_values = jnp.dot(
        sequence_standardized.reshape(local_sequence_total * local_position_total, feature_number),
        query_value_matrices.reshape(feature_number, heads_here * 4 * head_dim),
        preferred_element_type=jnp.float32,
    )
    linear_mapped_values = linear_mapped_values.astype(jnp.bfloat16).reshape(
        local_sequence_total, local_position_total, heads_here, 4 * head_dim
    )
    absent_target_penalty = ((1 - sequence_presence).astype(jnp.float32) * MASKED_FILL).astype(
        jnp.bfloat16
    )
    moved_proj, moved_bias = in_one_piece(
        (linear_mapped_values, absent_target_penalty), "col", 0, 1, 2
    )

    def attend_row(input_arrays):
        row_proj, row_bias = input_arrays
        query_part = row_proj[..., :head_dim]
        key_part = row_proj[..., head_dim : 2 * head_dim]
        value_part = row_proj[..., 2 * head_dim : 3 * head_dim]
        gate_part = row_proj[..., 3 * head_dim :]
        scores = (
            jnp.einsum("ihd,jhd->hij", query_part, key_part, preferred_element_type=jnp.float32)
            * score_scale
        )
        scores = scores + plane_float + row_bias.astype(jnp.float32)[None, None, :]
        weights = jax.nn.softmax(scores, axis=-1).astype(jnp.bfloat16)
        attended = jnp.einsum(
            "hij,jhd->ihd", weights, value_part, preferred_element_type=jnp.float32
        )
        return (jax.nn.sigmoid(gate_part.astype(jnp.float32)) * attended).astype(jnp.bfloat16)

    gated_rows = lax.map(attend_row, (moved_proj, moved_bias))
    gated = lax.all_to_all(gated_rows, "col", split_axis=1, concat_axis=0, tiled=True)
    sequence_matrix_flat = sequence_matrix.reshape(
        local_sequence_total * local_position_total, feature_number
    )
    all_gated, all_out = gather_packed((gated, merging_matrix), "head", (2, 0))
    full_update = jnp.dot(
        all_gated.reshape(local_sequence_total * local_position_total, -1),
        all_out,
        preferred_element_type=jnp.float32,
    )
    sequence_refreshed = (
        (sequence_matrix_flat.astype(jnp.float32) + full_update)
        .astype(jnp.bfloat16)
        .reshape(local_sequence_total, local_position_total, feature_number)
    )
    mask_as_float = sequence_presence.astype(jnp.float32)
    mask_lower_precision = sequence_presence.astype(jnp.bfloat16)
    tensor_average_standardized = standardize_features(
        sequence_refreshed, tensor_average_scaling
    ).astype(jnp.bfloat16)
    factor_vectors = jnp.dot(
        tensor_average_standardized.reshape(
            local_sequence_total * local_position_total, feature_number
        ),
        factor_mapping_matrix,
        preferred_element_type=jnp.float32,
    )
    factor_vectors = (
        factor_vectors.reshape(local_sequence_total, local_position_total, -1)
        * mask_as_float[..., None]
    ).astype(jnp.bfloat16)
    factor_width = factor_vectors.shape[2] // 2
    left_part = factor_vectors[..., :factor_width]
    right_part = factor_vectors[..., factor_width:]
    left_all, mask_all = in_one_piece_2((left_part, mask_lower_precision), "col", 1, 2)
    left_rows, mask_rows = in_one_piece((left_all, mask_all), SEQ, 1, 0, 2)
    flat_left = left_rows.reshape(left_rows.shape[0], tile_rows * factor_width)
    quarter = tile_cols // lax.axis_size("head")
    offset = lax.axis_index("head") * quarter
    right_slice = lax.dynamic_slice_in_dim(right_part, offset, quarter, 1).reshape(
        local_sequence_total, quarter * factor_width
    )
    mask_slice = lax.dynamic_slice_in_dim(mask_lower_precision, offset, quarter, 1)
    contract = (((0,), (0,)), ((), ()))
    right_piece, mask_piece = sent_together((right_slice, mask_slice), SEQ, 0, 1)
    outer_acc = lax.dot_general(
        flat_left, right_piece, contract, preferred_element_type=jnp.float32
    )
    count_acc = lax.dot_general(mask_rows, mask_piece, contract, preferred_element_type=jnp.float32)
    outer_sum = outer_acc.reshape(tile_rows, factor_width, quarter, factor_width).transpose(
        0, 2, 1, 3
    )
    outer_sum = outer_sum.reshape(tile_rows * quarter, factor_width * factor_width).astype(
        jnp.bfloat16
    )
    projected_pair = jnp.dot(outer_sum, tensor_average_matrix, preferred_element_type=jnp.float32)
    pair_keep = (
        lax.dynamic_slice_in_dim(couple_delta_selector, offset, quarter, 1)
        .astype(jnp.float32)
        .reshape(-1, 1)
    )
    pair_update = projected_pair / (1.0 + count_acc.reshape(-1, 1)) * pair_keep
    pair_slice = lax.dynamic_slice_in_dim(couple_matrix, offset, quarter, 1).reshape(
        tile_rows * quarter, pair_width
    )
    new_slice = (
        (pair_slice.astype(jnp.float32) + pair_update)
        .astype(jnp.bfloat16)
        .reshape(tile_rows, quarter, pair_width)
    )
    pair_output = collect(new_slice, "head", 1)
    return (sequence_refreshed, pair_output)


def solution(mesh):
    torus = Mesh(
        mesh.devices.reshape(2, 4, mesh.shape["col"], mesh.shape["head"]),
        ("seq_0", "seq_1", "col", "head"),
    )
    placed = (
        P(SEQ, "col", None),
        P(SEQ, "col"),
        P(SEQ, "col", None),
        P(SEQ, "col"),
        P(),
        P(),
        P(None, "head"),
        P(None, "head", None),
        P("head", None),
        P(),
        P(),
        P(),
    )
    return jax.shard_map(
        local,
        mesh=torus,
        in_specs=placed,
        out_specs=(P(SEQ, "col", None), P(SEQ, "col", None)),
        check_vma=False,
    )
```

profile of v0, /device:TPU:1, one launch (start us, length us, event | category | flops | bytes accessed | tf_op | source)
XLA Modules:
  0.0 294.4 jit_solution(7864498606571112478)
XLA Ops:
  7.3 1.5 convert_reduce_fusion
  8.8 1.7 fusion.12
  10.5 1.6 fusion.14
  12.2 0.2 convolution_convert_fusion
  12.6 5.5 %all-gather = bf16[4,64,32]{1,2,0:T(8,128)(2,1)S(1)} all-gather(bf16[2,64,32]{1,2,0:T(8,128)(2,1)S(1)} %copy.64), channel_id=2, replica_groups=mesh['seq_0'=2,'seq_1'=4,'col'=16,'head'=4] {'seq_0'}, dimensions={0}, use_global_device_ids=true | all-gather | bytes 24576 | tf_op jit(solution)/shard_map/all_gather | solution.py:26
  18.1 10.2 %all-gather.1 = bf16[8,1,2,64,32]{3,4,2,1,0:T(8,128)(2,1)} all-gather(bf16[2,1,2,64,32]{3,4,2,1,0:T(8,128)(2,1)S(1)} %bitcast.137), channel_id=3, replica_groups=mesh['seq_0'=2,'seq_1'=4,'col'=16,'head'=4] {'seq_1'}, dimensions={0}, use_global_device_ids=true | all-gather | bytes 81920 | tf_op jit(solution)/shard_map/all_gather | solution.py:26
  28.6 0.3 multiply_reduce_fusion
  28.8 0.2 copy.62
  29.1 0.2 multiply_convert_fusion
  29.3 0.2 convolution_convert_fusion.1
  29.6 31.0 %all_to_all.44 = bf16[16,32,257]{2,1,0:T(8,128)(2,1)S(1)} all-to-all(bf16[16,32,257]{2,1,0:T(8,128)(2,1)S(1)} %pad_maximum_fusion), channel_id=1, replica_groups=mesh['seq_0'=2,'seq_1'=4,'col'=16,'head'=4] {'col'}, dimensions={0} | all-to-all | bytes 526336 | tf_op jit(solution)/shard_map/all_to_all | solution.py:41
  60.8 44.6 %all-gather.6.cloned.1.call-done = bf16[64,2,1,2,64,32]{4,5,3,2,1,0:T(8,128)(2,1)} async-done(((bf16[4,2,1,2,64,32]{4,5,3,2,1,0:T(8,128)(2,1)}), bf16[64,2,1,2,64,32]{4,5,3,2,1,0:T(8,128)(2,1)}) %all-gather.6.cloned.1.call-update) | async-done | bytes 1048592 | tf_op jit(solution)/shard_map/all_gather | solution.py:26
  105.4 2.2 convert_bitcast_fusion
  107.5 0.8 copy.67
  108.4 5.7 %copy.68 = f32[2,8,64,16,32]{2,1,4,3,0:T(8,128)} copy(f32[2,8,64,16,32]{2,4,0,3,1:T(8,128)S(1)} %bitcast.113) | data formatting | bytes 4194304 | tf_op jit(solution)/shard_map/convert_element_type | solution.py:137
  114.1 3.4 %reshape.165 = f32[2,512,512]{1,2,0:T(8,128)S(1)} reshape(f32[2,8,64,16,32]{2,1,4,3,0:T(8,128)} %copy.68) | data formatting | bytes 4194304 | tf_op jit(solution)/shard_map/convert_element_type | solution.py:137
  117.5 0.5 add_add_fusion
  118.1 1.3 copy-done.1
  119.4 0.5 fusion.32
  119.9 2.8 fusion.11
  122.9 0.9 reshape.178
  123.8 7.6 %all-to-all-start.1 = ((bf16[16,2,1024]{2,1,0:T(2,128)(2,1)}), bf16[16,2,1024]{2,1,0:T(2,128)(2,1)S(1)}, u32[]{:S(2)}, u32[]{:S(2)}) async-start(bf16[16,2,1024]{2,1,0:T(2,128)(2,1)} %reshape.178), calls=%async_computation.1 | async-start | bytes 131072 | tf_op jit(solution)/shard_map/all_to_all | solution.py:174
  131.5 0.2 copy.72
  131.7 0.7 dynamic-slice_convert_fusion
  132.6 10.3 %all-to-all-done.1 = bf16[16,2,1024]{2,1,0:T(2,128)(2,1)S(1)} async-done(((bf16[16,2,1024]{2,1,0:T(2,128)(2,1)}), bf16[16,2,1024]{2,1,0:T(2,128)(2,1)S(1)}, u32[]{:S(2)}, u32[]{:S(2)}) %all-to-all-start.1) | async-done | bytes 65568 | tf_op jit(solution)/shard_map/all_to_all | solution.py:174
  143.0 0.2 reshape.179
  143.3 16.6 %all-gather.3 = bf16[196608]{0:T(1024)(128)(2,1)S(1)} all-gather(bf16[49152]{0:T(1024)(128)(2,1)S(1)} %pad_maximum_fusion.2), channel_id=5, replica_groups=mesh['seq_0'=2,'seq_1'=4,'col'=16,'head'=4] {'head'}, dimensions={0}, use_global_device_ids=true | all-gather | bytes 491520 | tf_op jit(solution)/shard_map/all_gather | solution.py:54
  160.3 0.6 reshape.157
  160.9 1.2 copy.71
  162.1 1.0 reshape_reshape.10
  163.2 0.4 convert_reduce_fusion.1
  163.6 0.2 fusion.17
  163.8 0.2 fusion.19
  164.1 0.2 fusion.6
  164.5 36.7 %all_gather.34 = bf16[16,512,33]{2,1,0:T(8,128)(2,1)S(1)} all-gather(bf16[16,32,33]{2,1,0:T(8,128)(2,1)S(1)} %pad_maximum_fusion.1), channel_id=1, replica_groups=mesh['seq_0'=2,'seq_1'=4,'col'=16,'head'=4] {'col'}, dimensions={1}, use_global_device_ids=true | all-gather | bytes 574464 | tf_op jit(solution)/shard_map/all_gather | solution.py:67
  201.3 1.4 copy.92
  202.6 4.5 %reshape.180 = bf16[8,2,16896]{2,1,0:T(2,128)(2,1)} reshape(bf16[512,16,33]{2,1,0:T(8,128)(2,1)S(1)} %bitcast.115) | data formatting | bytes 1081344
  207.1 5.8 %all-to-all-start.2 = ((bf16[8,2,16896]{2,1,0:T(2,128)(2,1)}), bf16[8,2,16896]{2,1,0:T(2,128)(2,1)S(1)}, u32[]{:S(2)}, u32[]{:S(2)}) async-start(bf16[8,2,16896]{2,1,0:T(2,128)(2,1)} %reshape.180), calls=%async_computation.2 | async-start | bytes 1081344 | tf_op jit(solution)/shard_map/all_to_all | solution.py:41
  213.0 31.1 %all_gather.35 = bf16[128,264]{1,0:T(8,128)(2,1)S(1)} all-gather(bf16[16,264]{1,0:T(8,128)(2,1)S(1)} %pad_maximum_fusion.3), channel_id=1, replica_groups=mesh['seq_0'=2,'seq_1'=4,'col'=16,'head'=4] {'seq_0','seq_1'}, dimensions={0}, use_global_device_ids=true | all-gather | bytes 76032 | tf_op jit(solution)/shard_map/all_gather | solution.py:78
  244.0 0.7 copy.76
  244.8 5.4 %reshape.181 = bf16[512,16,33]{2,1,0:T(8,128)(2,1)S(1)} reshape(bf16[8,2,16896]{2,1,0:T(2,128)(2,1)S(1)} %all-to-all-done.2) | data formatting | bytes 1081344
  250.2 3.2 %copy.74 = bf16[16,8,64,33]{2,0,1,3:T(8,128)(2,1)S(1)} copy(bf16[16,8,64,33]{3,0,2,1:T(8,128)(2,1)S(1)} %bitcast.114) | data formatting | bytes 1081344 | tf_op jit(solution)/shard_map/all_to_all | solution.py:41
  253.7 0.8 copy.75
  254.6 3.2 %convert_bitcast_fusion.1 = bf16[64,8,32,32]{3,2,1,0:T(8,128)(2,1)} fusion(bf16[8,32,128,1]{2,1,0,3:T(8,128)(2,1)S(1)} %bitcast.134, bf16[128,64,32]{0,2,1:T(8,128)(2,1)S(1)} %copy.75), kind=kOutput, calls=%fused_computation.2 | convolution fusion | flops 134742016 | bytes 1638400 | tf_op jit(solution)/shard_map/dot_general | solution.py:219
  257.8 6.2 %convert_element_type.141 = bf16[512,1024]{1,0:T(8,128)(2,1)S(1)} reshape(bf16[64,8,32,32]{3,2,1,0:T(8,128)(2,1)} %convert_bitcast_fusion.1) | data formatting | bytes 2097152 | tf_op jit(solution)/shard_map/convert_element_type | solution.py:226
  264.1 1.4 fusion.9
  265.6 21.1 %all_to_all.45 = bf16[4,64,8,128]{3,2,1,0:T(8,128)(2,1)S(1)} all-to-all(bf16[4,64,8,128]{3,2,1,0:T(8,128)(2,1)S(1)} %broadcast_in_dim.17), channel_id=1, replica_groups=mesh['seq_0'=2,'seq_1'=4,'col'=16,'head'=4] {'head'}, dimensions={0} | all-to-all | bytes 1048576 | tf_op jit(solution)/shard_map/all_to_all | solution.py:83
  286.7 0.9 copy.91
  (63 shorter events, 2.6 us)
Async XLA Ops:
  7.2 257.0 %copy-start = (bf16[1024,128]{1,0:T(8,128)(2,1)S(1)}, bf16[1024,128]{1,0:T(8,128)(2,1)}, u32[]{:S(2)}) copy-start(bf16[1024,128]{1,0:T(8,128)(2,1)} %param.23) | copy-start | bytes 786436
  7.2 5.0 %copy-start.11 = (bf16[128,2]{0,1:T(2,128)(2,1)S(1)}, bf16[128,2]{0,1:T(2,128)(2,1)}, u32[]{:S(2)}) copy-start(bf16[128,2]{0,1:T(2,128)(2,1)} %param.18) | copy-start | bytes 1540
  7.2 21.2 %copy-start.7 = (s32[16,32]{1,0:T(8,128)S(1)}, s32[16,32]{1,0:T(8,128)}, u32[]{:S(2)}) copy-start(s32[16,32]{1,0:T(8,128)} %param.13) | copy-start | bytes 6148
  7.2 21.2 %copy-start.2 = (bf16[16,32,256]{2,1,0:T(8,128)(2,1)S(1)}, bf16[16,32,256]{2,1,0:T(8,128)(2,1)}, u32[]{:S(2)}) copy-start(bf16[16,32,256]{2,1,0:T(8,128)(2,1)} %param.12) | copy-start | bytes 786436
  7.2 21.8 %copy-start.9 = (f32[256]{0:T(256)S(1)}, f32[256]{0:T(256)}, u32[]{:S(2)}) copy-start(f32[256]{0:T(256)} %param.16) | copy-start | bytes 3076
  7.2 98.2 %all-gather.6.cloned.1.call-start = ((), (), s32[]{:S(2)}) async-start(), calls=%async_computation.4 | async-start | bytes 2228224 | tf_op jit(solution)/shard_map/all_gather | solution.py:26
  8.7 20.5 %copy-start.5 = (bf16[256,2,128]{2,1,0:T(2,128)(2,1)S(1)}, bf16[256,2,128]{2,1,0:T(2,128)(2,1)}, u32[]{:S(2)}) copy-start(bf16[256,2,128]{2,1,0:T(2,128)(2,1)} %param.19) | copy-start | bytes 393220
  118.0 1.4 copy-start.1
  119.8 11.6 %copy-start.6 = (bf16[64,256]{1,0:T(8,128)(2,1)S(1)}, bf16[64,256]{1,0:T(8,128)(2,1)}, u32[]{:S(2)}) copy-start(bf16[64,256]{1,0:T(8,128)(2,1)} %param.20) | copy-start | bytes 98308
  123.8 19.2 %all-to-all-start.1 = ((bf16[16,2,1024]{2,1,0:T(2,128)(2,1)}), bf16[16,2,1024]{2,1,0:T(2,128)(2,1)S(1)}, u32[]{:S(2)}, u32[]{:S(2)}) async-start(bf16[16,2,1024]{2,1,0:T(2,128)(2,1)} %reshape.178), calls=%async_computation.1 | async-start | bytes 131072 | tf_op jit(solution)/shard_map/all_to_all | solution.py:174
  160.8 3.0 %copy-start.10 = (f32[256]{0:T(256)S(1)}, f32[256]{0:T(256)}, u32[]{:S(2)}) copy-start(f32[256]{0:T(256)} %param.21) | copy-start | bytes 3076
  162.1 2.0 copy-start.8
  163.6 1.0 copy-start.3
  207.1 37.7 %all-to-all-start.2 = ((bf16[8,2,16896]{2,1,0:T(2,128)(2,1)}), bf16[8,2,16896]{2,1,0:T(2,128)(2,1)S(1)}, u32[]{:S(2)}, u32[]{:S(2)}) async-start(bf16[8,2,16896]{2,1,0:T(2,128)(2,1)} %reshape.180), calls=%async_computation.2 | async-start | bytes 1081344 | tf_op jit(solution)/shard_map/all_to_all | solution.py:41
  253.4 1.1 copy-start.4
Sparse Core Ops, SparseCore 0:
  28.5 76.8 all-gather.5
where the time goes:
time: 295 us; the launch traced here: 294 us
  blocking collectives  152 us (52%)
  waiting for transfers between devices  55 us (19%)
  local copies, waits for them, and re-layouts  40.7 us (14%)
  between operations  14.5 us (5%)
  starting transfers between devices  13.4 us (5%)
  other arithmetic  9.48 us (3%)
  matrix products  9.12 us (3%)
    all_gather x1, waiting for transfers between devices, gather_in_order(): tiles = lax.all_gather(tiles, axes[k])  44.6 us
    all_gather x1, blocking collectives, in_one_piece_2(): whole = lax.all_gather(both, axis, axis=dim, tiled=True)  36.7 us
    all_gather x1, blocking collectives, sent_together(): lax.all_gather(both, axis, axis=dim, tiled=True)  31.1 us
    all_to_all x1, blocking collectives, in_one_piece(): lax.all_to_all(both, axis, split_axis=split_dim, concat_axis=concat_dim,...  31 us
    all_to_all x1, blocking collectives, copy_for_each(): lax.all_to_all(jnp.broadcast_to(value[None], (length, *value.shape)), axi...  21.1 us
    all_gather x1, blocking collectives, gather_packed(): lines, at, finished = (lax.all_gather(vector, axis), 0, [])  16.6 us
    all_gather x2, blocking collectives, gather_in_order(): tiles = lax.all_gather(tiles, axes[k])  15.8 us
    unnamed x29, local copies, waits for them, and re-layouts  12.4 us
  transfers between devices with their start and end apart: 3, of which 2 were waited for; matrix products, arithmetic and copies ran while one was open for 1% of the time, Pallas kernels for 0%

commit v1 on v0

v1 whole, which is shorter than its diff:
```python
import jax
import jax.numpy as jnp
from jax import lax
from jax.experimental import pallas as pl
from jax.experimental.pallas import tpu as pltpu
from jax.sharding import Mesh
from jax.sharding import PartitionSpec as P

SEQ = ("seq_0", "seq_1")
EPSILON = 1e-05
MASKED_FILL = -1000000000.0
F32 = jnp.float32
BF16 = jnp.bfloat16

SEQS, COLS, HEADS = 8, 16, 4
ROWS, POS, WIDTH = 16, 32, 256
TILE_I, TILE_J, PAIR = 64, 32, 128
ALL_POS = COLS * POS
OWN_POS = ALL_POS // HEADS
D = 32


def iota(shape, dim):
    return lax.broadcasted_iota(jnp.int32, shape, dim)


def dot(a, b):
    return jnp.dot(a, b, preferred_element_type=F32)


def dot_first(a, b):
    return lax.dot_general(a, b, (((0,), (0,)), ((), ())), preferred_element_type=F32)


def one_hot(mask):
    return mask.astype(F32).astype(BF16)


def normed(values, gain, width):
    average = jnp.sum(values, axis=-1, keepdims=True) * (1.0 / width)
    centered = values - average
    variance = jnp.sum(centered * centered, axis=-1, keepdims=True) * (1.0 / width)
    return centered * lax.rsqrt(variance + EPSILON) * gain


def vmem_call(kernel, out_shapes, *args, scalars=(), scratch=(), flops=1000000, name=None):
    specs = [pl.BlockSpec(memory_space=pltpu.SMEM)] * len(scalars)
    specs += [pl.BlockSpec(memory_space=pltpu.VMEM)] * len(args)
    single = not isinstance(out_shapes, (list, tuple))
    shapes = [out_shapes] if single else list(out_shapes)
    found = pl.pallas_call(
        kernel,
        out_shape=shapes,
        in_specs=specs,
        out_specs=[pl.BlockSpec(memory_space=pltpu.VMEM)] * len(shapes),
        scratch_shapes=list(scratch),
        cost_estimate=pl.CostEstimate(flops=flops, bytes_accessed=1000000, transcendentals=0),
        compiler_params=pltpu.CompilerParams(vmem_limit_bytes=48 * 1024 * 1024),
        name=name,
    )(*scalars, *args)
    return found[0] if single else found


def shape_of(dims, dtype=BF16):
    return jax.ShapeDtypeStruct(dims, dtype)


Z1_ROWS = 2 * POS + TILE_J + ROWS


def first_kernel(place, msa, presence, couple, gain, logits, out):
    col = place[0]
    low_lane = iota((PAIR, PAIR), 1) < TILE_I
    columns = logits[...].astype(F32)
    spread = jnp.where(low_lane, columns[:, 0:1], columns[:, 1:2]).astype(BF16)
    pair_gain = gain[...]
    step = 8
    place_of_lane = iota((TILE_J, PAIR), 1) % TILE_I

    def body(k, total):
        block = couple[pl.ds(k * step, step)].astype(F32).reshape(step * TILE_J, PAIR)
        value = normed(block, pair_gain, PAIR).astype(BF16)
        found = dot(value, spread)
        for r in range(step):
            row = found[r * TILE_J : (r + 1) * TILE_J]
            total = total + jnp.where(place_of_lane == k * step + r, row, 0.0)
        return total

    bias = lax.fori_loop(0, TILE_I // step, body, jnp.zeros((TILE_J, PAIR), F32))
    bias = bias.astype(BF16)
    marks = presence[...].astype(F32)
    marks = jnp.concatenate([marks] * 4, axis=1)
    marks = jnp.where(iota((ROWS, PAIR), 1) // POS == col % 4, marks, 0.0).astype(BF16)
    out[:, 0:POS, :] = msa[:, :, 0:128]
    out[:, POS : 2 * POS, :] = msa[:, :, 128:256]
    for dest in range(COLS):
        out[dest, 2 * POS : 2 * POS + TILE_J, :] = bias
        out[dest, 2 * POS + TILE_J :, :] = marks


def present_tile(first, t):
    at = 2 * POS + TILE_J
    total = first[4 * t, at:, :].astype(F32)
    for k in range(1, 4):
        total = total + first[4 * t + k, at:, :].astype(F32)
    return total.astype(BF16)


S1_ROWS = ALL_POS + 4 * ROWS


def spread_kernel(first, out):
    strip = first[:, 2 * POS : 2 * POS + TILE_J, :].reshape(ALL_POS, PAIR)
    tiles = [present_tile(first, t) for t in range(4)]
    for dest in range(SEQS):
        out[dest, 0:ALL_POS, :] = strip
        for t in range(4):
            out[dest, ALL_POS + ROWS * t : ALL_POS + ROWS * (t + 1), :] = tiles[t]


H1_ROWS = OWN_POS // 2 + 2 * 2 * D


def attend_kernel(place, first, strips, weights, gain, merging, keep, out, residual, marks, factor):
    seq, col, head = place[0], place[1], place[2]
    raw = jnp.concatenate(
        [
            first[:, 0:POS, :].reshape(ALL_POS, 128),
            first[:, POS : 2 * POS, :].reshape(ALL_POS, 128),
        ],
        axis=1,
    ).astype(F32)
    standard = normed(raw, gain[...], WIDTH).astype(BF16)
    both = jnp.concatenate([weights[0], weights[1]], axis=1)
    projected = dot(standard, both)
    rounded = projected.astype(BF16)
    turned = rounded.astype(F32).T

    own_row = one_hot(iota((ROWS, 128), 0) == col)
    row_marks = jnp.concatenate(
        [dot_first(present_tile(first, t), own_row) for t in range(4)], axis=0
    )
    key_bias = ((1.0 - row_marks) * MASKED_FILL).astype(BF16).astype(F32)

    by_owner = raw.reshape(COLS, HEADS, 8, WIDTH)
    marks_by_owner = row_marks.reshape(COLS, HEADS, 8, 128)
    own = jnp.zeros((COLS, 8, WIDTH), F32)
    own_marks = jnp.zeros((COLS, 8, 128), F32)
    for k in range(HEADS):
        own = own + jnp.where(head == k, by_owner[:, k], 0.0)
        own_marks = own_marks + jnp.where(head == k, marks_by_owner[:, k], 0.0)
    residual[...] = own.reshape(OWN_POS, WIDTH).astype(BF16)
    marks[...] = own_marks.reshape(OWN_POS, 128)

    rows_i = jnp.zeros((SEQS * ROWS, TILE_I), F32)
    rows_j = jnp.zeros((SEQS * ROWS, TILE_J), F32)
    for t in range(4):
        at = ALL_POS + ROWS * t
        tile = strips[:, at : at + ROWS, :].reshape(SEQS * ROWS, 128)
        lane = iota((128, TILE_I), 0) + 128 * t
        rows_i = rows_i + dot(tile, one_hot(lane == seq * TILE_I + iota((128, TILE_I), 1)))
        lane = iota((128, TILE_J), 0) + 128 * t
        rows_j = rows_j + dot(tile, one_hot(lane == col * TILE_J + iota((128, TILE_J), 1)))
    count = dot_first(rows_j.astype(BF16), rows_i.astype(BF16))
    same = one_hot(iota((TILE_I, TILE_I), 0) == iota((TILE_I, TILE_I), 1))
    kept = dot_first(keep[...].astype(F32).astype(BF16), same)
    factor[...] = kept / (1.0 + count)

    score_scale = D ** (-0.5)
    low = iota((D, 128), 1) < TILE_I
    zero = jnp.zeros((D, 128), F32)
    values = jnp.concatenate([turned[2 * D : 3 * D], turned[6 * D : 7 * D]], axis=0).astype(BF16)

    def tile_attended(a, first_queries, second_queries):
        queries = jnp.concatenate(
            [
                zero,
                jnp.where(low, first_queries, 0.0),
                zero,
                zero,
                zero,
                jnp.where(low, 0.0, second_queries),
                zero,
                zero,
            ],
            axis=0,
        ).astype(BF16)
        scores = dot(rounded, queries) * score_scale
        scores = scores + strips[a, 0:ALL_POS, :].astype(F32) + key_bias
        top = jnp.max(scores, axis=0, keepdims=True)
        raised = jnp.exp(scores - top)
        shares = (raised / jnp.sum(raised, axis=0, keepdims=True)).astype(BF16)
        return dot(values, shares)

    pieces = []
    for t in range(4):
        at = slice(128 * t, 128 * (t + 1))
        q0, q1 = turned[0:D, at], turned[4 * D : 5 * D, at]
        even = tile_attended(2 * t, q0, pltpu.roll(q1, 64, 1))
        odd = tile_attended(2 * t + 1, pltpu.roll(q0, 64, 1), q1)
        head_0 = jnp.where(low, even[0:D], pltpu.roll(odd[0:D], 64, 1))
        head_1 = jnp.where(low, pltpu.roll(even[D:], 64, 1), odd[D:])
        gate = jnp.concatenate([turned[3 * D : 4 * D, at], turned[7 * D : 8 * D, at]], axis=0)
        attended = jnp.concatenate([head_0, head_1], axis=0)
        pieces.append(jax.nn.sigmoid(gate) * attended)
    gated = jnp.concatenate(pieces, axis=1)
    gated = jnp.concatenate([gated, jnp.zeros_like(gated)], axis=0).T
    gated = gated.reshape(COLS // 2, 2, HEADS, 8, 128)
    for k in range(HEADS):
        even = gated[:, 0, k].reshape(OWN_POS // 2, 128)
        odd = gated[:, 1, k].reshape(OWN_POS // 2, 128)
        out[k, 0 : OWN_POS // 2, :] = (even + pltpu.roll(odd, 64, 1)).astype(BF16)
        out[k, OWN_POS // 2 : OWN_POS // 2 + 2 * D, :] = merging[:, 0:128]
        out[k, OWN_POS // 2 + 2 * D :, :] = merging[:, 128:256]


Z2_ROWS = 64


def finish_kernel(heads, residual, marks, gain, mapping, out):
    half = OWN_POS // 2
    gated = jnp.concatenate([heads[k, 0:half, :] for k in range(HEADS)], axis=1)
    empty = jnp.zeros((2 * D, WIDTH), BF16)
    blocks = [
        jnp.concatenate([heads[k, half : half + 2 * D, :], heads[k, half + 2 * D :, :]], axis=1)
        for k in range(HEADS)
    ]
    even_rows, odd_rows = [], []
    for block in blocks:
        even_rows += [block, empty]
        odd_rows += [empty, block]
    even = dot(gated, jnp.concatenate(even_rows, axis=0)).reshape(COLS // 2, 1, 8, WIDTH)
    odd = dot(gated, jnp.concatenate(odd_rows, axis=0)).reshape(COLS // 2, 1, 8, WIDTH)
    update = jnp.concatenate([even, odd], axis=1).reshape(OWN_POS, WIDTH)
    refreshed = (residual[...].astype(F32) + update).astype(BF16).astype(F32)
    standard = normed(refreshed, gain[...], WIDTH).astype(BF16)
    factors = (dot(standard, mapping[...]) * marks[:, 0:64]).astype(BF16)

    lane = iota((2 * D, 128), 1)
    source = iota((2 * D, 128), 0)
    position = iota((OWN_POS, 128), 0)
    place = iota((OWN_POS, 128), 1)
    left = dot(factors, one_hot(source == lane % D))
    left = jnp.where(position % 4 == place // D, left, 0.0).astype(BF16)
    left = dot(one_hot(iota((32, OWN_POS), 1) // 4 == iota((32, OWN_POS), 0)), left).astype(BF16)
    right = jnp.zeros((COLS * 16, 128), F32)
    chosen = iota((COLS * 16, OWN_POS), 0)
    block_of = iota((COLS * 16, OWN_POS), 1) // 8
    for k in range(2):
        part = dot(factors, one_hot(source == D + 16 * k + lane // 8))
        part = jnp.where(position % 8 == place % 8, part, 0.0).astype(BF16)
        right = right + dot(one_hot((chosen // 16 == block_of) & (chosen % 16 == k)), part)
    rows = jnp.concatenate(
        [
            refreshed[:, 0:128].reshape(COLS, 8, 128),
            refreshed[:, 128:256].reshape(COLS, 8, 128),
        ],
        axis=1,
    ).astype(BF16)
    for dest in range(COLS):
        out[dest, 0:32, :] = left
    out[:, 32:48, :] = rows
    out[:, 48:64, :] = right.reshape(COLS, 16, 128).astype(BF16)


S2_ROWS = 96


def turn_kernel(second, out, refreshed):
    left = second[:, 0:32, :].reshape(32 * ROWS, 128)
    to, source = iota((512, 512), 0), iota((512, 512), 1)
    left = dot(one_hot((source // 32 == to % 16) & (source % 32 == to // 16)), left).astype(BF16)
    right = second[:, 48:64, :].reshape(16 * ROWS, 128)
    to, source = iota((32, 256), 0), iota((32, 256), 1)
    right = dot(one_hot((source // 16 == to % 16) & (source % 16 == to // 16)), right).astype(BF16)
    for dest in range(SEQS):
        out[dest, 0:64, :] = left[64 * dest : 64 * (dest + 1)]
        out[dest, 64:96, :] = right
    refreshed[...] = second[:, 32:48, :].reshape(ROWS * 16, 128)


H2_ROWS = SEQS * S2_ROWS + ROWS * 16


def copies_kernel(third, refreshed, out):
    for dest in range(HEADS):
        out[dest, 0 : SEQS * S2_ROWS, :] = third[...].reshape(SEQS * S2_ROWS, 128)
        out[dest, SEQS * S2_ROWS :, :] = refreshed[...]


def outer_kernel(last, couple, factor, matrix, sequence_out, pair_out, outer, mixed):
    at = SEQS * S2_ROWS
    low, high = [], []
    for h in range(HEADS):
        rows = last[h, at:, :].astype(F32).reshape(ROWS, 16, 128)
        low.append(rows[:, 0:8])
        high.append(rows[:, 8:16])
    sequence_out[:, :, 0:128] = jnp.concatenate(low, axis=1).astype(BF16)
    sequence_out[:, :, 128:256] = jnp.concatenate(high, axis=1).astype(BF16)

    def gathered(h, row):
        return jnp.concatenate(
            [last[h, S2_ROWS * a + row : S2_ROWS * a + row + ROWS, :] for a in range(SEQS)], axis=0
        )

    mixed[...] = jnp.zeros_like(mixed)
    for q in range(D):
        block = matrix[q]
        for k in range(4):
            mixed[128 * q + D * k : 128 * q + D * (k + 1), 128 * k : 128 * (k + 1)] = block

    left = jnp.concatenate(
        [gathered(h, ROWS * g) for h in range(HEADS) for g in range(4)], axis=1
    )
    for k in range(2):
        found = [dot_first(gathered(h, 64 + ROWS * k), left) for h in range(HEADS)]
        for q in range(16):
            block = jnp.concatenate([f[8 * q : 8 * (q + 1)] for f in found], axis=0).astype(BF16)
            channel = 16 * k + q
            for n in range(16):
                outer[TILE_J * n : TILE_J * (n + 1), 128 * channel : 128 * (channel + 1)] = block[
                    :, 128 * n : 128 * (n + 1)
                ]
    total = dot(outer[...], mixed[...])
    for n in range(16):
        for k in range(4):
            i = 32 * (n % 4 // 2) + 8 * (n // 4) + 4 * (n % 2) + k
            update = total[TILE_J * n : TILE_J * (n + 1), 128 * k : 128 * (k + 1)]
            update = update * factor[:, i : i + 1]
            pair_out[i] = (couple[i].astype(F32) + update).astype(BF16)


def local(
    sequence_matrix,
    sequence_presence,
    couple_matrix,
    couple_delta_selector,
    softmax_scaling_vector,
    couple_scaling_vector,
    couple_logit_matrix,
    query_value_matrices,
    merging_matrix,
    tensor_average_scaling,
    factor_mapping_matrix,
    tensor_average_matrix,
):
    assert sequence_matrix.shape == (ROWS, POS, WIDTH)
    assert couple_matrix.shape == (TILE_I, TILE_J, PAIR)
    seq, col, head = lax.axis_index(SEQ), lax.axis_index("col"), lax.axis_index("head")
    place = jnp.stack([seq, col, head]).astype(jnp.int32)
    first = vmem_call(
        first_kernel,
        shape_of((COLS, Z1_ROWS, 128)),
        sequence_matrix,
        sequence_presence,
        couple_matrix,
        couple_scaling_vector.reshape(1, PAIR),
        couple_logit_matrix,
        scalars=(place[1:2],),
        name="first",
    )
    first = lax.all_to_all(first, "col", 0, 0, tiled=True)
    strips = vmem_call(spread_kernel, shape_of((SEQS, S1_ROWS, 128)), first, name="spread")
    strips = lax.all_to_all(strips, SEQ, 0, 0, tiled=True)
    heads, residual, marks, factor = vmem_call(
        attend_kernel,
        (
            shape_of((HEADS, H1_ROWS, 128)),
            shape_of((OWN_POS, WIDTH)),
            shape_of((OWN_POS, 128), F32),
            shape_of((TILE_J, TILE_I), F32),
        ),
        first,
        strips,
        query_value_matrices.transpose(1, 0, 2),
        softmax_scaling_vector.reshape(1, WIDTH),
        merging_matrix,
        couple_delta_selector,
        scalars=(place,),
        name="attend",
    )
    heads = lax.all_to_all(heads, "head", 0, 0, tiled=True)
    second = vmem_call(
        finish_kernel,
        shape_of((COLS, Z2_ROWS, 128)),
        heads,
        residual,
        marks,
        tensor_average_scaling.reshape(1, WIDTH),
        factor_mapping_matrix,
        name="finish",
    )
    second = lax.all_to_all(second, "col", 0, 0, tiled=True)
    third, refreshed = vmem_call(
        turn_kernel,
        (shape_of((SEQS, S2_ROWS, 128)), shape_of((ROWS * 16, 128))),
        second,
        name="turn",
    )
    third = lax.all_to_all(third, SEQ, 0, 0, tiled=True)
    last = vmem_call(copies_kernel, shape_of((HEADS, H2_ROWS, 128)), third, refreshed, name="copies")
    last = lax.all_to_all(last, "head", 0, 0, tiled=True)
    return tuple(
        vmem_call(
            outer_kernel,
            (shape_of((ROWS, POS, WIDTH)), shape_of((TILE_I, TILE_J, PAIR))),
            last,
            couple_matrix,
            factor,
            tensor_average_matrix.reshape(D, D, PAIR).swapaxes(0, 1),
            scratch=(
                pltpu.VMEM((16 * TILE_J, D * 128), BF16),
                pltpu.VMEM((D * 128, 4 * PAIR), BF16),
            ),
            name="outer",
        )
    )


def solution(mesh):
    torus = Mesh(
        mesh.devices.reshape(2, 4, mesh.shape["col"], mesh.shape["head"]),
        ("seq_0", "seq_1", "col", "head"),
    )
    placed = (
        P(SEQ, "col", None),
        P(SEQ, "col"),
        P(SEQ, "col", None),
        P(SEQ, "col"),
        P(),
        P(),
        P(None, "head"),
        P(None, "head", None),
        P("head", None),
        P(),
        P(),
        P(),
    )
    return jax.shard_map(
        local,
        mesh=torus,
        in_specs=placed,
        out_specs=(P(SEQ, "col", None), P(SEQ, "col", None)),
        check_vma=False,
    )
```

time: 295 us -> 150 us (0.51)
  blocking collectives: 152 us -> 68.7 us
  local copies, waits for them, and re-layouts: 40.7 us -> 4.48 us
  waiting for transfers between devices: 55 us -> 29.7 us
  starting transfers between devices: 13.4 us -> 30.6 us
  Pallas kernels: 0 us -> 15.3 us
  between operations: 14.5 us -> 0.71 us
  other arithmetic: 9.48 us -> 0.08 us
  matrix products: 9.12 us -> 0 us
    all_gather x5 -> x0, blocking collectives: 100 us -> none  [the longest x1 36.7 us: in_one_piece_2(): whole = lax.all_gather(both, axis, axis=dim, tiled=True)]
    all_gather x1 -> x0, waiting for transfers between devices: 44.6 us -> none  [gather_in_order(): tiles = lax.all_gather(tiles, axes[k])]
    all_to_all x2 -> x3, waiting for transfers between devices: 10.4 us -> 29.7 us  [the longest x1 13.4 us: local(): last = lax.all_to_all(last, 'head', 0, 0, tiled=True)]
    all_to_all x2 -> x3, starting transfers between devices: 13.4 us -> 30.6 us  [the longest x1 12 us: local(): last = lax.all_to_all(last, 'head', 0, 0, tiled=True)]
    all_to_all x2 -> x3, blocking collectives: 52.1 us -> 68.7 us  [the longest x1 36.4 us: local(): first = lax.all_to_all(first, 'col', 0, 0, tiled=True)]
    convert_element_type x5 -> x0, local copies, waits for them, and re-layouts: 16.2 us -> none  [the longest x3 9.98 us: local(): plane_float = bias_plane.astype(jnp.float32)]
    pallas_call x0 -> x7, Pallas kernels: none -> 15.3 us  [vmem_call(): pl.pallas_call(kernel, out_shape=shapes, in_specs=specs, out_specs=[pl.Bl...]
    dot_general x9 -> x0, matrix products: 9.12 us -> none  [the longest x1 3.19 us: local(): lax.dot_general(flat_left, right_piece, contract, preferred_element_type=...]
  transfers between devices with their start and end apart: 3 -> 3, of which waited for: 2 -> 3; matrix products, arithmetic and copies ran while one was open for 1% -> 0% of each run, Pallas kernels for 0% -> 0%
where the time goes in v1:
time: 150 us
  blocking collectives  68.7 us (46%)
  starting transfers between devices  30.6 us (20%)
  waiting for transfers between devices  29.7 us (20%)
  Pallas kernels  15.3 us (10%)
  local copies, waits for them, and re-layouts  4.48 us (3%)
    all_to_all x1, blocking collectives, local(): first = lax.all_to_all(first, 'col', 0, 0, tiled=True)  36.4 us
    all_to_all x1, blocking collectives, local(): second = lax.all_to_all(second, 'col', 0, 0, tiled=True)  22.6 us
    pallas_call x7, Pallas kernels, vmem_call(): pl.pallas_call(kernel, out_shape=shapes, in_specs=specs, out_specs=[pl.Bl...  15.3 us
    all_to_all x1, waiting for transfers between devices, local(): last = lax.all_to_all(last, 'head', 0, 0, tiled=True)  13.4 us
    all_to_all x1, waiting for transfers between devices, local(): strips = lax.all_to_all(strips, SEQ, 0, 0, tiled=True)  12.4 us
    all_to_all x1, starting transfers between devices, local(): last = lax.all_to_all(last, 'head', 0, 0, tiled=True)  12 us
    all_to_all x1, starting transfers between devices, local(): heads = lax.all_to_all(heads, 'head', 0, 0, tiled=True)  11.8 us
    all_to_all x1, blocking collectives, local(): third = lax.all_to_all(third, SEQ, 0, 0, tiled=True)  9.69 us
  transfers between devices with their start and end apart: 3, of which 3 were waited for; matrix products, arithmetic and copies ran while one was open for 0% of the time, Pallas kernels for 0%

profile of v1, /device:TPU:1, one launch (start us, length us, event | category | flops | bytes accessed | tf_op | source)
XLA Modules:
  0.0 149.6 jit_solution(7698765211699127894)
XLA Ops:
  0.6 0.8 copy.18.logits
  1.4 0.0 copy-start
  1.4 1.0 copy-done
  2.5 0.0 copy-start.2
  2.5 0.9 copy-done.2
  3.4 0.0 copy-start.4
  3.4 0.7 copy-done.4
  4.1 0.0 copy-start.7
  4.1 0.7 copy-done.7
  4.8 2.7 %first.1 = bf16[16,112,128]{2,1,0:T(8,128)(2,1)S(1)} custom-call(s32[1]{0:T(128)} %bitcast.1.place, bf16[16,32,256]{2,1,0:T(8,128)(2,1)S(1)} %copy-done.2, s32[16,32]{1,0:T(8,128)S(1)} %copy-done.4, bf16[64,32,128]{2,1,0:T(8,128)(2,1)S(1)} %copy-done, f32[1,128]{1,0:T(1,128)S(1)} %bitcast.17, bf16[128,2]{1,0:T(8,128)(2,1)S(1)} %copy.18.logits), custom_call_target="tpu_custom_call" | custom-call | flops 1000000 | bytes 1000000 | tf_op jit(solution)/shard_map/first/pallas_call | solution.py:51
  7.5 36.4 %all_to_all.30.first = bf16[16,112,128]{2,1,0:T(8,128)(2,1)S(1)} all-to-all(bf16[16,112,128]{2,1,0:T(8,128)(2,1)S(1)} %first.1), channel_id=1, replica_groups=mesh['seq_0'=2,'seq_1'=4,'col'=16,'head'=4] {'col'}, dimensions={0} | all-to-all | bytes 917504 | tf_op jit(solution)/shard_map/all_to_all | solution.py:362
  43.8 1.2 spread.1
  45.0 0.0 copy-start.9
  45.0 0.0 copy-start.11
  45.0 0.0 copy-start.3
  45.0 0.0 copy-start.5
  45.1 6.8 %all-to-all-start.1 = ((bf16[8,576,128]{2,1,0:T(8,128)(2,1)}), bf16[8,576,128]{2,1,0:T(8,128)(2,1)S(1)}, u32[]{:S(2)}, u32[]{:S(2)}) async-start(bf16[8,576,128]{2,1,0:T(8,128)(2,1)} %spread.1), calls=%async_computation.1 | async-start | bytes 2359296 | tf_op jit(solution)/shard_map/all_to_all | solution.py:364
  51.8 0.0 copy-done.9
  51.9 0.0 copy-done.11
  51.9 0.0 copy-start.10
  51.9 0.1 copy.20.keep
  52.0 0.0 copy-start.6
  52.0 0.1 pad_add_fusion.place
  52.1 12.4 %all-to-all-done.1.strips = bf16[8,576,128]{2,1,0:T(8,128)(2,1)S(1)} async-done(((bf16[8,576,128]{2,1,0:T(8,128)(2,1)}), bf16[8,576,128]{2,1,0:T(8,128)(2,1)S(1)}, u32[]{:S(2)}, u32[]{:S(2)}) %all-to-all-start.1) | async-done | bytes 1179680 | tf_op jit(solution)/shard_map/all_to_all | solution.py:364
  64.5 0.0 copy-done.3
  64.5 0.0 copy-done.5
  64.5 4.7 %attend.1 = (bf16[4,192,128]{2,1,0:T(8,128)(2,1)}, bf16[128,256]{1,0:T(8,128)(2,1)S(1)}, f32[128,128]{1,0:T(8,128)S(1)}, f32[32,64]{1,0:T(8,128)S(1)}) custom-call(s32[3]{0:T(128)S(1)} %pad_add_fusion.place, bf16[16,112,128]{2,1,0:T(8,128)(2,1)S(1)} %all_to_all.30.first, bf16[8,576,128]{2,1,0:T(8,128)(2,1)S(1)} %all-to-all-done.1.strips, ...), custom_call_target="tpu_custom_call" | custom-call | flops 1000000 | bytes 1000000 | tf_op jit(solution)/shard_map/attend/pallas_call | solution.py:51
  69.2 11.8 %all-to-all-start.2 = ((bf16[4,192,128]{2,1,0:T(8,128)(2,1)}), bf16[4,192,128]{2,1,0:T(8,128)(2,1)S(1)}, u32[]{:S(2)}, u32[]{:S(2)}) async-start(bf16[4,192,128]{2,1,0:T(8,128)(2,1)} %get-tuple-element.8), calls=%async_computation.2 | async-start | bytes 393216 | tf_op jit(solution)/shard_map/all_to_all | solution.py:382
  81.0 0.0 copy-done.10
  81.0 0.1 copy.21.mapping
  81.1 4.0 %all-to-all-done.2.heads = bf16[4,192,128]{2,1,0:T(8,128)(2,1)S(1)} async-done(((bf16[4,192,128]{2,1,0:T(8,128)(2,1)}), bf16[4,192,128]{2,1,0:T(8,128)(2,1)S(1)}, u32[]{:S(2)}, u32[]{:S(2)}) %all-to-all-start.2) | async-done | bytes 196640 | tf_op jit(solution)/shard_map/all_to_all | solution.py:382
  85.1 0.0 copy-done.6
  85.1 0.9 finish.1
  86.0 22.6 %all_to_all.31.second = bf16[16,64,128]{2,1,0:T(8,128)(2,1)S(1)} all-to-all(bf16[16,64,128]{2,1,0:T(8,128)(2,1)S(1)} %finish.1), channel_id=1, replica_groups=mesh['seq_0'=2,'seq_1'=4,'col'=16,'head'=4] {'col'}, dimensions={0} | all-to-all | bytes 524288 | tf_op jit(solution)/shard_map/all_to_all | solution.py:393
  108.7 0.3 turn.1
  109.0 9.7 %all_to_all.32.third = bf16[8,96,128]{2,1,0:T(8,128)(2,1)S(1)} all-to-all(bf16[8,96,128]{2,1,0:T(8,128)(2,1)S(1)} %get-tuple-element.11), channel_id=1, replica_groups=mesh['seq_0'=2,'seq_1'=4,'col'=16,'head'=4] {'seq_0','seq_1'}, dimensions={0} | all-to-all | bytes 393216 | tf_op jit(solution)/shard_map/all_to_all | solution.py:400
  118.7 1.1 copies.1
  119.8 0.0 copy-start.8
  119.8 0.0 copy-start.1
  119.8 12.0 %all-to-all-start.5 = ((bf16[4,1024,128]{2,1,0:T(8,128)(2,1)}), bf16[4,1024,128]{2,1,0:T(8,128)(2,1)S(1)}, u32[]{:S(2)}, u32[]{:S(2)}) async-start(bf16[4,1024,128]{2,1,0:T(8,128)(2,1)} %copies.1), calls=%async_computation.5 | async-start | bytes 2097152 | tf_op jit(solution)/shard_map/all_to_all | solution.py:402
  131.8 0.0 copy-done.8
  131.8 0.1 copy.25
  131.9 13.4 %all-to-all-done.5.last = bf16[4,1024,128]{2,1,0:T(8,128)(2,1)S(1)} async-done(((bf16[4,1024,128]{2,1,0:T(8,128)(2,1)}), bf16[4,1024,128]{2,1,0:T(8,128)(2,1)S(1)}, u32[]{:S(2)}, u32[]{:S(2)}) %all-to-all-start.5) | async-done | bytes 1048608 | tf_op jit(solution)/shard_map/all_to_all | solution.py:402
  145.2 0.0 copy-done.1
  145.2 4.4 %outer.1 = (bf16[16,32,256]{2,1,0:T(8,128)(2,1)}, bf16[64,32,128]{2,1,0:T(8,128)(2,1)}) custom-call(bf16[4,1024,128]{2,1,0:T(8,128)(2,1)S(1)} %all-to-all-done.5.last, bf16[64,32,128]{2,1,0:T(8,128)(2,1)S(1)} %copy-done.1, f32[32,64]{1,0:T(8,128)S(1)} %get-tuple-element.13.factor, bf16[32,32,128]{2,1,0:T(8,128)(2,1)S(1)} %bitcast.13), custom_call_target="tpu_custom_call" | custom-call | flops 1000000 | bytes 1000000 | tf_op jit(solution)/shard_map/outer/pallas_call | solution.py:51
  (1 shorter events, 0.0 us)
Async XLA Ops:
  1.4 1.0 copy-start
  2.5 0.9 copy-start.2
  3.4 0.7 copy-start.4
  4.1 0.7 copy-start.7
  45.0 6.8 %copy-start.9 = (bf16[256,2,128]{2,1,0:T(2,128)(2,1)S(1)}, bf16[256,2,128]{2,1,0:T(2,128)(2,1)}, u32[]{:S(2)}) copy-start(bf16[256,2,128]{2,1,0:T(2,128)(2,1)} %param.19) | copy-start | bytes 393220
  45.0 6.8 %copy-start.11 = (s32[64,32]{0,1:T(8,128)S(1)}, s32[64,32]{0,1:T(8,128)}, u32[]{:S(2)}) copy-start(s32[64,32]{0,1:T(8,128)} %param.15) | copy-start | bytes 24580
  45.0 19.4 %copy-start.3 = (bf16[64,256]{1,0:T(8,128)(2,1)S(1)}, bf16[64,256]{1,0:T(8,128)(2,1)}, u32[]{:S(2)}) copy-start(bf16[64,256]{1,0:T(8,128)(2,1)} %merging.1) | copy-start | bytes 98308
  45.0 19.4 %copy-start.5 = (f32[256]{0:T(256)S(1)}, f32[256]{0:T(256)}, u32[]{:S(2)}) copy-start(f32[256]{0:T(256)} %param.16) | copy-start | bytes 3076
  45.1 19.4 %all-to-all-start.1 = ((bf16[8,576,128]{2,1,0:T(8,128)(2,1)}), bf16[8,576,128]{2,1,0:T(8,128)(2,1)S(1)}, u32[]{:S(2)}, u32[]{:S(2)}) async-start(bf16[8,576,128]{2,1,0:T(8,128)(2,1)} %spread.1), calls=%async_computation.1 | async-start | bytes 2359296 | tf_op jit(solution)/shard_map/all_to_all | solution.py:364
  51.9 29.1 %copy-start.10 = (bf16[256,64]{0,1:T(8,128)(2,1)S(1)}, bf16[256,64]{0,1:T(8,128)(2,1)}, u32[]{:S(2)}) copy-start(bf16[256,64]{0,1:T(8,128)(2,1)} %param.22) | copy-start | bytes 98308
  52.0 33.1 %copy-start.6 = (f32[256]{0:T(256)S(1)}, f32[256]{0:T(256)}, u32[]{:S(2)}) copy-start(f32[256]{0:T(256)} %param.21) | copy-start | bytes 3076
  69.2 15.9 %all-to-all-start.2 = ((bf16[4,192,128]{2,1,0:T(8,128)(2,1)}), bf16[4,192,128]{2,1,0:T(8,128)(2,1)S(1)}, u32[]{:S(2)}, u32[]{:S(2)}) async-start(bf16[4,192,128]{2,1,0:T(8,128)(2,1)} %get-tuple-element.8), calls=%async_computation.2 | async-start | bytes 393216 | tf_op jit(solution)/shard_map/all_to_all | solution.py:382
  119.8 12.0 %copy-start.8 = (bf16[1024,128]{1,0:T(8,128)(2,1)S(1)}, bf16[1024,128]{1,0:T(8,128)(2,1)}, u32[]{:S(2)}) copy-start(bf16[1024,128]{1,0:T(8,128)(2,1)} %param.23) | copy-start | bytes 786436
  119.8 25.5 %copy-start.1 = (bf16[64,32,128]{2,1,0:T(8,128)(2,1)S(1)}, bf16[64,32,128]{2,1,0:T(8,128)(2,1)}, u32[]{:S(2)}) copy-start(bf16[64,32,128]{2,1,0:T(8,128)(2,1)} %couple.3) | copy-start | bytes 1572868
  119.8 25.5 %all-to-all-start.5 = ((bf16[4,1024,128]{2,1,0:T(8,128)(2,1)}), bf16[4,1024,128]{2,1,0:T(8,128)(2,1)S(1)}, u32[]{:S(2)}, u32[]{:S(2)}) async-start(bf16[4,1024,128]{2,1,0:T(8,128)(2,1)} %copies.1), calls=%async_computation.5 | async-start | bytes 2097152 | tf_op jit(solution)/shard_map/all_to_all | solution.py:402

commit v2 on v1

v2 whole, which is shorter than its diff:
```python
import jax
import jax.numpy as jnp
from jax import lax
from jax.experimental import pallas as pl
from jax.experimental.pallas import tpu as pltpu
from jax.sharding import Mesh
from jax.sharding import PartitionSpec as P

SEQ = ("seq_0", "seq_1")
EPSILON = 1e-05
MASKED_FILL = -1000000000.0
F32 = jnp.float32
BF16 = jnp.bfloat16

SEQS, COLS, HEADS = 8, 16, 4
ROWS, POS, WIDTH = 16, 32, 256
TILE_I, TILE_J, PAIR = 64, 32, 128
ALL_POS = COLS * POS
OWN_POS = ALL_POS // HEADS
D = 32


def iota(shape, dim):
    return lax.broadcasted_iota(jnp.int32, shape, dim)


def dot(a, b):
    return jnp.dot(a, b, preferred_element_type=F32)


def dot_first(a, b):
    return lax.dot_general(a, b, (((0,), (0,)), ((), ())), preferred_element_type=F32)


def dot_last(a, b):
    return lax.dot_general(a, b, (((1,), (1,)), ((), ())), preferred_element_type=F32)


def one_hot(mask):
    return mask.astype(F32).astype(BF16)


def normed(values, gain, width):
    average = jnp.sum(values, axis=-1, keepdims=True) * (1.0 / width)
    centered = values - average
    variance = jnp.sum(centered * centered, axis=-1, keepdims=True) * (1.0 / width)
    return centered * lax.rsqrt(variance + EPSILON) * gain


def vmem_call(
    kernel, out_shapes, *args, hbm=(), scratch=(), flops=1000000, name=None, vmem=48
):
    specs = [pl.BlockSpec(memory_space=pltpu.HBM)] * len(hbm)
    specs += [pl.BlockSpec(memory_space=pltpu.VMEM)] * len(args)
    single = not isinstance(out_shapes, (list, tuple))
    shapes = [out_shapes] if single else list(out_shapes)
    found = pl.pallas_call(
        kernel,
        out_shape=shapes,
        in_specs=specs,
        out_specs=[pl.BlockSpec(memory_space=pltpu.VMEM)] * len(shapes),
        scratch_shapes=list(scratch),
        cost_estimate=pl.CostEstimate(flops=flops, bytes_accessed=1000000, transcendentals=0),
        compiler_params=pltpu.CompilerParams(vmem_limit_bytes=vmem * 1024 * 1024 - 65536),
        name=name,
    )(*hbm, *args)
    return found[0] if single else found


def to_partner(value, distance):
    return lax.ppermute(value, "head", [(k, k ^ distance) for k in range(HEADS)])


def shape_of(dims, dtype=BF16):
    return jax.ShapeDtypeStruct(dims, dtype)


HALF = POS // 2
Z1_MARKS = 2 * HALF + TILE_J
Z1_ROWS = Z1_MARKS + 8


def first_kernel(msa_hbm, presence_hbm, couple_hbm, gain_hbm, logits_hbm, out, msa, presence, couple, gain, logits, sems):
    pairs = (
        (logits_hbm, logits),
        (presence_hbm, presence),
        (gain_hbm, gain),
        (couple_hbm, couple),
        (msa_hbm, msa),
    )
    copies = [pltpu.make_async_copy(x, y, sems.at[k]) for k, (x, y) in enumerate(pairs)]
    for copy in copies:
        copy.start()
    low_row = iota((PAIR, PAIR), 0) < TILE_I
    copies[0].wait()
    rows = logits[...].astype(F32)
    spread = jnp.where(low_row, rows[0:1, :], rows[1:2, :]).astype(BF16)
    place_of_lane = iota((TILE_J, PAIR), 1) % TILE_I
    step = 16

    copies[1].wait()
    marks = presence[...].astype(F32)
    marks = jnp.concatenate([marks] * 4, axis=1)
    marks = jnp.where(iota((ROWS, PAIR), 1) // POS == iota((ROWS, PAIR), 0) % 4, marks, 0.0)
    marks = dot(one_hot(iota((8, ROWS), 1) // 4 == iota((8, ROWS), 0)), marks.astype(BF16))
    marks = marks.astype(BF16)
    copies[2].wait()
    copies[3].wait()
    pair_gain = gain[...]

    def body(k, total):
        block = couple[pl.ds(k * step, step)].astype(F32).reshape(step * TILE_J, PAIR)
        value = normed(block, pair_gain, PAIR).astype(BF16)
        found = dot_last(value, spread)
        for r in range(step):
            row = found[r * TILE_J : (r + 1) * TILE_J]
            total = total + jnp.where(place_of_lane == k * step + r, row, 0.0)
        return total

    bias = jnp.zeros((TILE_J, PAIR), F32)
    for k in range(TILE_I // step):
        bias = body(k, bias)
    bias = bias.astype(BF16)
    copies[4].wait()
    core = lax.axis_index("head") % 2
    for k in range(2):

        @pl.when(core == k)
        def _():
            out[:, 0:HALF, :] = msa[:, HALF * k : HALF * (k + 1), 0:128]
            out[:, HALF : 2 * HALF, :] = msa[:, HALF * k : HALF * (k + 1), 128:256]

    for dest in range(COLS):
        out[dest, 2 * HALF : Z1_MARKS, :] = bias
        out[dest, Z1_MARKS:, :] = marks


S1_ROWS = ALL_POS + 24


def spread_kernel(first, out, raw):
    strip = first[:, 2 * HALF : Z1_MARKS, :].reshape(ALL_POS, PAIR)
    columns = first[lax.axis_index("col"), Z1_MARKS:, :]
    for dest in range(SEQS):
        out[dest, 0:ALL_POS, :] = strip
        out[dest, ALL_POS : ALL_POS + 8, :] = first[2 * dest, Z1_MARKS:, :]
        out[dest, ALL_POS + 8 : ALL_POS + 16, :] = first[2 * dest + 1, Z1_MARKS:, :]
        out[dest, ALL_POS + 16 :, :] = columns
    raw[...] = first[:, 0 : 2 * HALF, :].reshape(COLS * 2 * HALF, 128)


def by_index(arrived, head, k):
    bits = [(k ^ d) == head for d in range(1, HEADS)]
    block = arrived[0]
    for d in range(1, HEADS):
        block = jnp.where(bits[d - 1], arrived[d], block)
    return block


def project_kernel(
    first, raw, raw_1, weights, gain, rounded_out, turned_out, key_bias, own_marks, residual
):
    col, head = lax.axis_index("col"), lax.axis_index("head")
    own_half, other_half = raw[...].astype(F32), raw_1[...].astype(F32)
    low, high = [], []
    for k in range(2):
        rows = jnp.where(head % 2 == k, own_half, other_half).reshape(COLS, 1, 2 * HALF, 128)
        low.append(rows[:, :, 0:HALF])
        high.append(rows[:, :, HALF:])
    low = jnp.concatenate(low, axis=1).reshape(ALL_POS, 128)
    high = jnp.concatenate(high, axis=1).reshape(ALL_POS, 128)
    rows = jnp.concatenate([low, high], axis=1)
    by_owner = rows.reshape(COLS, HEADS, 8, WIDTH)
    own = jnp.zeros((COLS, 8, WIDTH), F32)
    for k in range(HEADS):
        own = own + jnp.where(head == k, by_owner[:, k], 0.0)
    residual[...] = own.reshape(OWN_POS, WIDTH).astype(BF16)
    standard = normed(rows, gain[...], WIDTH).astype(BF16)
    both = jnp.concatenate([weights[0], weights[1]], axis=1)
    rounded = dot(standard, both).astype(BF16)
    rounded_out[...] = rounded
    turned_out[...] = rounded.astype(F32).T.astype(BF16)

    packed = first[:, Z1_MARKS:, :].reshape(COLS * 8, 128)
    shape = (COLS, COLS * 8)
    picked = dot(one_hot(iota(shape, 1) == iota(shape, 0) * 8 + col // 4), packed).astype(BF16)
    shape = (128, POS)
    picked = dot(picked, one_hot(iota(shape, 0) == POS * (col % 4) + iota(shape, 1))).astype(BF16)
    shape = (ALL_POS, COLS)
    picked = dot(one_hot(iota(shape, 0) // POS == iota(shape, 1)), picked)
    shape = (ALL_POS, POS)
    picked = jnp.where(iota(shape, 0) % POS == iota(shape, 1), picked, 0.0).astype(BF16)
    marks = dot(picked, jnp.ones((POS, 128), BF16))
    key_bias[...] = ((1.0 - marks) * MASKED_FILL).astype(BF16)
    by_owner = marks.reshape(COLS, HEADS, 8, 128)
    own = jnp.zeros((COLS, 8, 128), F32)
    for k in range(HEADS):
        own = own + jnp.where(head == k, by_owner[:, k], 0.0)
    own_marks[...] = own.reshape(OWN_POS, 128)


def count_kernel(strips, keep, factor):
    def presence(k):
        at = ALL_POS + 8 * k
        return strips[:, at : at + 8, :].reshape(SEQS * 8, 128)

    first_rows, second_rows, columns = presence(0), presence(1), presence(2)
    count = jnp.zeros((TILE_J, TILE_I), F32)
    for k in range(4):
        shape = (128, TILE_I)
        lane, place = iota(shape, 0) - POS * k, iota(shape, 1)
        rows = dot(first_rows, one_hot((lane == place) & (place < POS)))
        rows = rows + dot(second_rows, one_hot((lane == place - POS) & (place >= POS)))
        shape = (128, TILE_J)
        found = dot(columns, one_hot(iota(shape, 0) - POS * k == iota(shape, 1)))
        count = count + dot_first(found.astype(BF16), rows.astype(BF16))
    same = one_hot(iota((TILE_I, TILE_I), 0) == iota((TILE_I, TILE_I), 1))
    kept = dot_first(keep[...].astype(F32).astype(BF16), same)
    factor[...] = kept / (1.0 + count)


H1_ROWS = OWN_POS // 2 + 2 * 2 * D


def attend_kernel(strips, rounded_in, turned_in, key_bias_in, merging, out):
    rounded = rounded_in[...]
    turned = turned_in[...].astype(F32)
    key_bias = key_bias_in[...].astype(F32)
    score_scale = D ** (-0.5)
    low = iota((D, 128), 1) < TILE_I
    zero = jnp.zeros((D, 128), F32)
    values = jnp.concatenate([turned[2 * D : 3 * D], turned[6 * D : 7 * D]], axis=0).astype(BF16)

    def tile_attended(a, first_queries, second_queries):
        queries = jnp.concatenate(
            [
                zero,
                jnp.where(low, first_queries, 0.0),
                zero,
                zero,
                zero,
                jnp.where(low, 0.0, second_queries),
                zero,
                zero,
            ],
            axis=0,
        ).astype(BF16)
        scores = dot(rounded, queries) * score_scale
        scores = scores + strips[a, 0:ALL_POS, :].astype(F32) + key_bias
        top = jnp.max(scores, axis=0, keepdims=True)
        raised = jnp.exp(scores - top)
        shares = (raised / jnp.sum(raised, axis=0, keepdims=True)).astype(BF16)
        return dot(values, shares)

    pieces = []
    for t in range(4):
        at = slice(128 * t, 128 * (t + 1))
        q0, q1 = turned[0:D, at], turned[4 * D : 5 * D, at]
        even = tile_attended(2 * t, q0, pltpu.roll(q1, 64, 1))
        odd = tile_attended(2 * t + 1, pltpu.roll(q0, 64, 1), q1)
        head_0 = jnp.where(low, even[0:D], pltpu.roll(odd[0:D], 64, 1))
        head_1 = jnp.where(low, pltpu.roll(even[D:], 64, 1), odd[D:])
        gate = jnp.concatenate([turned[3 * D : 4 * D, at], turned[7 * D : 8 * D, at]], axis=0)
        attended = jnp.concatenate([head_0, head_1], axis=0)
        pieces.append(jax.nn.sigmoid(gate) * attended)
    gated = jnp.concatenate(pieces, axis=1)
    gated = jnp.concatenate([gated, jnp.zeros_like(gated)], axis=0).T
    gated = gated.reshape(COLS // 2, 2, HEADS, 8, 128)
    for k in range(HEADS):
        even = gated[:, 0, k].reshape(OWN_POS // 2, 128)
        odd = gated[:, 1, k].reshape(OWN_POS // 2, 128)
        out[k, 0 : OWN_POS // 2, :] = (even + pltpu.roll(odd, 64, 1)).astype(BF16)
        out[k, OWN_POS // 2 : OWN_POS // 2 + 2 * D, :] = merging[:, 0:128]
        out[k, OWN_POS // 2 + 2 * D :, :] = merging[:, 128:256]


Z2_ROWS = 56


def finish_kernel(heads, residual, marks, gain, mapping, out):
    half = OWN_POS // 2
    gated = jnp.concatenate([heads[k, 0:half, :] for k in range(HEADS)], axis=1)
    empty = jnp.zeros((2 * D, WIDTH), BF16)
    blocks = [
        jnp.concatenate([heads[k, half : half + 2 * D, :], heads[k, half + 2 * D :, :]], axis=1)
        for k in range(HEADS)
    ]
    even_rows, odd_rows = [], []
    for block in blocks:
        even_rows += [block, empty]
        odd_rows += [empty, block]
    even = dot(gated, jnp.concatenate(even_rows, axis=0)).reshape(COLS // 2, 1, 8, WIDTH)
    odd = dot(gated, jnp.concatenate(odd_rows, axis=0)).reshape(COLS // 2, 1, 8, WIDTH)
    update = jnp.concatenate([even, odd], axis=1).reshape(OWN_POS, WIDTH)
    refreshed = (residual[...].astype(F32) + update).astype(BF16).astype(F32)
    standard = normed(refreshed, gain[...], WIDTH).astype(BF16)
    factors = (dot_last(standard, mapping[...]) * marks[:, 0:64]).astype(BF16)

    lane = iota((2 * D, 128), 1)
    source = iota((2 * D, 128), 0)
    position = iota((OWN_POS, 128), 0)
    place = iota((OWN_POS, 128), 1)
    left = dot(factors, one_hot(source == lane % D))
    left = jnp.where(position % 4 == place // D, left, 0.0).astype(BF16)
    left = dot(one_hot(iota((32, OWN_POS), 1) // 4 == iota((32, OWN_POS), 0)), left).astype(BF16)
    right = jnp.zeros((COLS * 8, 128), F32)
    chosen = iota((COLS * 8, OWN_POS), 0)
    block_of = iota((COLS * 8, OWN_POS), 1) // 8
    for k in range(2):
        part = dot(factors, one_hot(source == D + 16 * k + lane // 8))
        part = jnp.where(position % 8 == place % 8, part, 0.0).astype(BF16)
        right = right + dot(one_hot((chosen // 8 == block_of) & (chosen % 8 == k)), part)
    rows = jnp.concatenate(
        [
            refreshed[:, 0:128].reshape(COLS, 8, 128),
            refreshed[:, 128:256].reshape(COLS, 8, 128),
        ],
        axis=1,
    ).astype(BF16)
    for dest in range(COLS):
        out[dest, 0:32, :] = left
    out[:, 32:48, :] = rows
    out[:, 48:56, :] = right.reshape(COLS, 8, 128).astype(BF16)


S2_ROWS = 96
LAST_ROWS = SEQS * S2_ROWS + ROWS * 16


def join_kernel(third, refreshed, out):
    out[0 : SEQS * S2_ROWS, :] = third[...].reshape(SEQS * S2_ROWS, 128)
    out[SEQS * S2_ROWS :, :] = refreshed[...]


def turn_kernel(second, out, refreshed):
    left = second[:, 0:32, :].reshape(32 * ROWS, 128)
    to, source = iota((512, 512), 0), iota((512, 512), 1)
    left = dot(one_hot((source // 32 == to % 16) & (source % 32 == to // 16)), left).astype(BF16)
    right = second[:, 48:56, :].reshape(8 * ROWS, 128)
    to, source = iota((32, 128), 0), iota((32, 128), 1)
    right = dot(one_hot((source // 8 == to % 16) & (source % 8 == to // 16)), right).astype(BF16)
    for dest in range(SEQS):
        out[dest, 0:64, :] = left[64 * dest : 64 * (dest + 1)]
        out[dest, 64:96, :] = right
    refreshed[...] = second[:, 32:48, :].reshape(ROWS * 16, 128)


def outer_kernel(*refs):
    last = refs[0:HEADS]
    couple, factor, matrix, sequence_out, pair_out, outer, mixed = refs[HEADS:]
    head = lax.axis_index("head")
    end = SEQS * S2_ROWS
    arrived = [r[end:, :].astype(F32) for r in last]
    low, high = [], []
    for k in range(HEADS):
        rows = by_index(arrived, head, k).reshape(ROWS, 16, 128)
        low.append(rows[:, 0:8])
        high.append(rows[:, 8:16])
    sequence_out[:, :, 0:128] = jnp.concatenate(low, axis=1).astype(BF16)
    sequence_out[:, :, 128:256] = jnp.concatenate(high, axis=1).astype(BF16)

    factors = [r[0:end, :] for r in last]
    factors = [by_index(factors, head, k) for k in range(HEADS)]

    def gathered(h, row):
        return jnp.concatenate(
            [factors[h][S2_ROWS * a + row : S2_ROWS * a + row + ROWS] for a in range(SEQS)], axis=0
        )

    mixed[...] = jnp.zeros_like(mixed)
    for q in range(D):
        block = matrix[q]
        for k in range(4):
            mixed[128 * q + D * k : 128 * q + D * (k + 1), 128 * k : 128 * (k + 1)] = block

    left = jnp.concatenate(
        [gathered(h, ROWS * g) for h in range(HEADS) for g in range(4)], axis=1
    )
    for k in range(2):
        found = [dot_first(gathered(h, 64 + ROWS * k), left) for h in range(HEADS)]
        for q in range(16):
            block = jnp.concatenate([f[8 * q : 8 * (q + 1)] for f in found], axis=0).astype(BF16)
            channel = 16 * k + q
            for n in range(16):
                outer[TILE_J * n : TILE_J * (n + 1), 128 * channel : 128 * (channel + 1)] = block[
                    :, 128 * n : 128 * (n + 1)
                ]
    total = dot(outer[...], mixed[...])
    for n in range(16):
        for k in range(4):
            i = 32 * (n % 4 // 2) + 8 * (n // 4) + 4 * (n % 2) + k
            update = total[TILE_J * n : TILE_J * (n + 1), 128 * k : 128 * (k + 1)]
            update = update * factor[:, i : i + 1]
            pair_out[i] = (couple[i].astype(F32) + update).astype(BF16)


def local(
    sequence_matrix,
    sequence_presence,
    couple_matrix,
    couple_delta_selector,
    softmax_scaling_vector,
    couple_scaling_vector,
    couple_logit_matrix,
    query_value_matrices,
    merging_matrix,
    tensor_average_scaling,
    factor_mapping_matrix,
    tensor_average_matrix,
):
    assert sequence_matrix.shape == (ROWS, POS, WIDTH)
    assert couple_matrix.shape == (TILE_I, TILE_J, PAIR)
    first = vmem_call(
        first_kernel,
        shape_of((COLS, Z1_ROWS, 128)),
        hbm=(
            sequence_matrix,
            sequence_presence,
            couple_matrix,
            couple_scaling_vector.reshape(1, PAIR),
            couple_logit_matrix.T,
        ),
        scratch=(
            pltpu.VMEM((ROWS, POS, WIDTH), BF16),
            pltpu.VMEM((ROWS, POS), jnp.int32),
            pltpu.VMEM((TILE_I, TILE_J, PAIR), BF16),
            pltpu.VMEM((1, PAIR), F32),
            pltpu.VMEM((2, PAIR), BF16),
            pltpu.SemaphoreType.DMA((5,)),
        ),
        vmem=64,
        name="first",
    )
    first = lax.all_to_all(first, "col", 0, 0, tiled=True)
    strips, raw = vmem_call(
        spread_kernel,
        (shape_of((SEQS, S1_ROWS, 128)), shape_of((COLS * 2 * HALF, 128))),
        first,
        name="spread",
    )
    raws = [raw, to_partner(raw, 1)]
    strips = lax.all_to_all(strips, SEQ, 0, 0, tiled=True)
    rounded, turned, key_bias, marks, residual = vmem_call(
        project_kernel,
        (
            shape_of((ALL_POS, WIDTH)),
            shape_of((WIDTH, ALL_POS)),
            shape_of((ALL_POS, 128)),
            shape_of((OWN_POS, 128), F32),
            shape_of((OWN_POS, WIDTH)),
        ),
        first,
        *raws,
        query_value_matrices.transpose(1, 0, 2),
        softmax_scaling_vector.reshape(1, WIDTH),
        flops=400000000,
        name="project",
    )
    heads = vmem_call(
        attend_kernel,
        shape_of((HEADS, H1_ROWS, 128)),
        strips,
        rounded,
        turned,
        key_bias,
        merging_matrix,
        flops=600000000,
        name="attend",
    )
    heads = lax.all_to_all(heads, "head", 0, 0, tiled=True)
    factor = vmem_call(
        count_kernel,
        shape_of((TILE_J, TILE_I), F32),
        strips,
        couple_delta_selector,
        flops=100000000,
        name="count",
    )
    second = vmem_call(
        finish_kernel,
        shape_of((COLS, Z2_ROWS, 128)),
        heads,
        residual,
        marks,
        tensor_average_scaling.reshape(1, WIDTH),
        factor_mapping_matrix.T,
        flops=100000000,
        name="finish",
    )
    second = lax.all_to_all(second, "col", 0, 0, tiled=True)
    third, refreshed = vmem_call(
        turn_kernel,
        (shape_of((SEQS, S2_ROWS, 128)), shape_of((ROWS * 16, 128))),
        second,
        name="turn",
    )
    third = lax.all_to_all(third, SEQ, 0, 0, tiled=True)
    last = vmem_call(join_kernel, shape_of((LAST_ROWS, 128)), third, refreshed, name="join")
    across = to_partner(last, 2)
    last = [last, to_partner(last, 1), across, to_partner(across, 1)]
    return tuple(
        vmem_call(
            outer_kernel,
            (shape_of((ROWS, POS, WIDTH)), shape_of((TILE_I, TILE_J, PAIR))),
            *last,
            couple_matrix,
            factor,
            tensor_average_matrix.reshape(D, D, PAIR).swapaxes(0, 1),
            scratch=(
                pltpu.VMEM((16 * TILE_J, D * 128), BF16),
                pltpu.VMEM((D * 128, 4 * PAIR), BF16),
            ),
            flops=2000000000,
            name="outer",
        )
    )


def solution(mesh):
    torus = Mesh(
        mesh.devices.reshape(2, 4, mesh.shape["col"], mesh.shape["head"]),
        ("seq_0", "seq_1", "col", "head"),
    )
    placed = (
        P(SEQ, "col", None),
        P(SEQ, "col"),
        P(SEQ, "col", None),
        P(SEQ, "col"),
        P(),
        P(),
        P(None, "head"),
        P(None, "head", None),
        P("head", None),
        P(),
        P(),
        P(),
    )
    return jax.shard_map(
        local,
        mesh=torus,
        in_specs=placed,
        out_specs=(P(SEQ, "col", None), P(SEQ, "col", None)),
        check_vma=False,
    )
```

time: 150 us -> 128 us (0.85)
  waiting for transfers between devices: 29.7 us -> 3.43 us
  blocking collectives: 68.7 us -> 76.7 us
  local copies, waits for them, and re-layouts: 4.48 us -> 0.23 us
  starting transfers between devices: 30.6 us -> 32.3 us
    ppermute x0 -> x4, starting transfers between devices: none -> 25.5 us  [to_partner(): lax.ppermute(value, 'head', [(k, k ^ distance) for k in range(HEADS)])]
    all_to_all x2 -> x0, starting transfers between devices: 23.8 us -> none  [the longest x1 12 us: local(): last = lax.all_to_all(last, 'head', 0, 0, tiled=True)]
    all_to_all x2 -> x0, waiting for transfers between devices: 17.3 us -> none  [the longest x1 13.4 us: local(): last = lax.all_to_all(last, 'head', 0, 0, tiled=True)]
    all_to_all x0 -> x1, blocking collectives: none -> 14.4 us  [local(): heads = lax.all_to_all(heads, 'head', 0, 0, tiled=True)]
    all_to_all x1, waiting for transfers between devices: 12.4 us -> 2.26 us  [local(): strips = lax.all_to_all(strips, SEQ, 0, 0, tiled=True)]
    all_to_all x1, blocking collectives: 36.4 us -> 29.9 us  [local(): first = lax.all_to_all(first, 'col', 0, 0, tiled=True)]
    unnamed x28 -> x18, local copies, waits for them, and re-layouts: 4.37 us -> 0.13 us
    pallas_call x7 -> x9, Pallas kernels: 15.3 us -> 14 us  [vmem_call(): pl.pallas_call(kernel, out_shape=shapes, in_specs=specs, out_specs=[pl.Bl...]
  transfers between devices with their start and end apart: 3 -> 5, of which waited for: 3 -> 4; matrix products, arithmetic and copies ran while one was open for 0% -> 0% of each run, Pallas kernels for 0% -> 1%
where the time goes in v2:
time: 128 us; the launch traced here: 127 us
  blocking collectives  76.7 us (60%)
  starting transfers between devices  32.3 us (25%)
  Pallas kernels  14 us (11%)
  waiting for transfers between devices  3.43 us (3%)
    all_to_all x1, blocking collectives, local(): first = lax.all_to_all(first, 'col', 0, 0, tiled=True)  29.9 us
    ppermute x4, starting transfers between devices, to_partner(): lax.ppermute(value, 'head', [(k, k ^ distance) for k in range(HEADS)])  25.5 us
    all_to_all x1, blocking collectives, local(): second = lax.all_to_all(second, 'col', 0, 0, tiled=True)  22.7 us
    all_to_all x1, blocking collectives, local(): heads = lax.all_to_all(heads, 'head', 0, 0, tiled=True)  14.4 us
    pallas_call x9, Pallas kernels, vmem_call(): pl.pallas_call(kernel, out_shape=shapes, in_specs=specs, out_specs=[pl.Bl...  14 us
    all_to_all x1, blocking collectives, local(): third = lax.all_to_all(third, SEQ, 0, 0, tiled=True)  9.69 us
    all_to_all x1, starting transfers between devices, local(): strips = lax.all_to_all(strips, SEQ, 0, 0, tiled=True)  6.78 us
  transfers between devices with their start and end apart: 5, of which 4 were waited for; matrix products, arithmetic and copies ran while one was open for 0% of the time, Pallas kernels for 1%

profile of v2, /device:TPU:1, one launch (start us, length us, event | category | flops | bytes accessed | tf_op | source)
XLA Modules:
  0.0 127.4 jit_solution(16873974991857097010)
XLA Ops:
  0.6 2.7 %first.1 = bf16[16,72,128]{2,1,0:T(8,128)(2,1)} custom-call(bf16[16,32,256]{2,1,0:T(8,128)(2,1)} %msa_hbm.1, s32[16,32]{1,0:T(8,128)} %presence_hbm.1, bf16[64,32,128]{2,1,0:T(8,128)(2,1)} %refs_4_.1, f32[1,128]{1,0:T(1,128)} %bitcast.18, bf16[2,128]{1,0:T(2,128)(2,1)} %bitcast.19), custom_call_target="tpu_custom_call" | custom-call | flops 1000000 | bytes 1000000 | tf_op jit(solution)/shard_map/first/pallas_call | solution.py:57
  3.3 29.9 %all_to_all.25.first = bf16[16,72,128]{2,1,0:T(8,128)(2,1)S(1)} all-to-all(bf16[16,72,128]{2,1,0:T(8,128)(2,1)} %first.1), channel_id=1, replica_groups=mesh['seq_0'=2,'seq_1'=4,'col'=16,'head'=4] {'col'}, dimensions={0} | all-to-all | bytes 589824 | tf_op jit(solution)/shard_map/all_to_all | solution.py:434
  33.2 1.1 spread.1
  34.4 0.0 copy-start.6
  34.4 0.0 copy-start.4
  34.4 6.8 %all-to-all-start.1 = ((bf16[8,536,128]{2,1,0:T(8,128)(2,1)}), bf16[8,536,128]{2,1,0:T(8,128)(2,1)S(1)}, u32[]{:S(2)}, u32[]{:S(2)}) async-start(bf16[8,536,128]{2,1,0:T(8,128)(2,1)} %get-tuple-element.11), calls=%async_computation.1 | async-start | bytes 2195456 | tf_op jit(solution)/shard_map/all_to_all | solution.py:442
  41.2 0.0 copy-start.3
  41.2 8.4 %collective-permute-start = (bf16[512,128]{1,0:T(8,128)(2,1)S(1)}, bf16[512,128]{1,0:T(8,128)(2,1)S(1)}, u32[]{:S(2)}, u32[]{:S(2)}) collective-permute-start(bf16[512,128]{1,0:T(8,128)(2,1)S(1)} %get-tuple-element.12.raw), channel_id=1, source_target_pairs={{0,1},{1,0},{2,3},{3,2},{4,5},{5,4},{6,7},{7,6},{8,9},{9,8},{10,11... | collective-permute-start | bytes 393224 | tf_op jit(solution)/shard_map/ppermute | solution.py:71
  49.5 0.0 copy-done.6
  49.6 0.9 collective-permute-done.raw_1
  50.5 0.0 copy-done.4
  50.5 0.6 project.1
  51.1 2.3 %all-to-all-done.1.strips = bf16[8,536,128]{2,1,0:T(8,128)(2,1)S(1)} async-done(((bf16[8,536,128]{2,1,0:T(8,128)(2,1)}), bf16[8,536,128]{2,1,0:T(8,128)(2,1)S(1)}, u32[]{:S(2)}, u32[]{:S(2)}) %all-to-all-start.1) | async-done | bytes 1097760 | tf_op jit(solution)/shard_map/all_to_all | solution.py:442
  53.4 0.0 copy-done.3
  53.4 0.0 copy-start.1
  53.4 0.0 copy-start.2
  53.4 3.0 %attend.1 = bf16[4,192,128]{2,1,0:T(8,128)(2,1)S(1)} custom-call(bf16[8,536,128]{2,1,0:T(8,128)(2,1)S(1)} %all-to-all-done.1.strips, bf16[512,256]{1,0:T(8,128)(2,1)S(1)} %get-tuple-element.13.rounded_in, bf16[256,512]{1,0:T(8,128)(2,1)S(1)} %get-tuple-element.14.turned_in, bf16[512,128]{1,0:T(8,128)(2,1)S(1)} %get-tuple-element.15.key_bias_in, ...), custom_call_target="tpu_custom_call" | custom-call | flops 600000000 | bytes 1000000 | tf_op jit(solution)/shard_map/attend/pallas_call | solution.py:57
  56.4 14.4 %all_to_all.26.heads = bf16[4,192,128]{2,1,0:T(8,128)(2,1)S(1)} all-to-all(bf16[4,192,128]{2,1,0:T(8,128)(2,1)S(1)} %attend.1), channel_id=1, replica_groups=mesh['seq_0'=2,'seq_1'=4,'col'=16,'head'=4] {'head'}, dimensions={0} | all-to-all | bytes 393216 | tf_op jit(solution)/shard_map/all_to_all | solution.py:470
  70.9 0.0 copy-done.1
  70.9 0.0 copy-done.2
  70.9 0.0 copy-start.7
  70.9 0.0 copy-start.5
  70.9 0.9 finish.1
  71.8 22.7 %all_to_all.27.second = bf16[16,56,128]{2,1,0:T(8,128)(2,1)S(1)} all-to-all(bf16[16,56,128]{2,1,0:T(8,128)(2,1)S(1)} %finish.1), channel_id=1, replica_groups=mesh['seq_0'=2,'seq_1'=4,'col'=16,'head'=4] {'col'}, dimensions={0} | all-to-all | bytes 458752 | tf_op jit(solution)/shard_map/all_to_all | solution.py:490
  94.5 0.3 turn.1
  94.8 9.7 %all_to_all.28.third = bf16[8,96,128]{2,1,0:T(8,128)(2,1)S(1)} all-to-all(bf16[8,96,128]{2,1,0:T(8,128)(2,1)S(1)} %get-tuple-element.18), channel_id=1, replica_groups=mesh['seq_0'=2,'seq_1'=4,'col'=16,'head'=4] {'seq_0','seq_1'}, dimensions={0} | all-to-all | bytes 393216 | tf_op jit(solution)/shard_map/all_to_all | solution.py:497
  104.5 0.0 copy-start
  104.5 2.1 %collective-permute-start.2 = (bf16[1024,128]{1,0:T(8,128)(2,1)S(1)}, bf16[1024,128]{1,0:T(8,128)(2,1)S(1)}, u32[]{:S(2)}, u32[]{:S(2)}) collective-permute-start(bf16[1024,128]{1,0:T(8,128)(2,1)S(1)} %join.1.refs_0_), channel_id=1, source_target_pairs={{0,2},{1,3},{2,0},{3,1},{4,6},{5,7},{6,4},{7,5},{8,10},{9,11},{10,... | collective-permute-start | bytes 786440 | tf_op jit(solution)/shard_map/ppermute | solution.py:71
  106.6 9.1 %collective-permute-start.1 = (bf16[1024,128]{1,0:T(8,128)(2,1)S(1)}, bf16[1024,128]{1,0:T(8,128)(2,1)S(1)}, u32[]{:S(2)}, u32[]{:S(2)}) collective-permute-start(bf16[1024,128]{1,0:T(8,128)(2,1)S(1)} %join.1.refs_0_), channel_id=1, source_target_pairs={{0,1},{1,0},{2,3},{3,2},{4,5},{5,4},{6,7},{7,6},{8,9},{9,8},{10,11... | collective-permute-start | bytes 786440 | tf_op jit(solution)/shard_map/ppermute | solution.py:71
  115.7 0.0 collective-permute-done.2.refs_2_
  115.7 6.0 %collective-permute-start.3 = (bf16[1024,128]{1,0:T(8,128)(2,1)S(1)}, bf16[1024,128]{1,0:T(8,128)(2,1)S(1)}, u32[]{:S(2)}, u32[]{:S(2)}) collective-permute-start(bf16[1024,128]{1,0:T(8,128)(2,1)S(1)} %collective-permute-done.2.refs_2_), channel_id=1, source_target_pairs={{0,1},{1,0},{2,3},{3,2},{4,5},{5,4},{6,7},{7,6},{8,9},{9,8},{10,11... | collective-permute-start | bytes 786440 | tf_op jit(solution)/shard_map/ppermute | solution.py:71
  121.7 0.0 copy-done.7
  121.7 0.1 copy.17.keep
  121.8 0.0 copy-done.5
  121.8 0.1 copy.21
  121.9 0.7 count.1.refs_5_
  122.6 0.1 collective-permute-done.1.refs_1_
  122.6 0.2 collective-permute-done.3.refs_3_
  122.8 0.0 copy-done
  122.8 4.6 %outer.1 = (bf16[16,32,256]{2,1,0:T(8,128)(2,1)}, bf16[64,32,128]{2,1,0:T(8,128)(2,1)}) custom-call(bf16[1024,128]{1,0:T(8,128)(2,1)S(1)} %join.1.refs_0_, bf16[1024,128]{1,0:T(8,128)(2,1)S(1)} %collective-permute-done.1.refs_1_, bf16[1024,128]{1,0:T(8,128)(2,1)S(1)} %collective-permute-done.2.refs_2_, bf16[1024,128]{1,0:T(8,128)(2,1)S(1)} %collective-permute-done.3.refs_3_, ...), custom_call_target="tpu_custom_call" | custom-call | flops 2000000000 | bytes 1000000 | tf_op jit(solution)/shard_map/outer/pallas_call | solution.py:57
  (2 shorter events, 0.0 us)
Async XLA Ops:
  34.4 15.2 %copy-start.6 = (bf16[256,2,128]{2,1,0:T(2,128)(2,1)S(1)}, bf16[256,2,128]{2,1,0:T(2,128)(2,1)}, u32[]{:S(2)}) copy-start(bf16[256,2,128]{2,1,0:T(2,128)(2,1)} %param.19) | copy-start | bytes 393220
  34.4 16.1 %copy-start.4 = (f32[256]{0:T(256)S(1)}, f32[256]{0:T(256)}, u32[]{:S(2)}) copy-start(f32[256]{0:T(256)} %param.16) | copy-start | bytes 3076
  34.4 19.0 %all-to-all-start.1 = ((bf16[8,536,128]{2,1,0:T(8,128)(2,1)}), bf16[8,536,128]{2,1,0:T(8,128)(2,1)S(1)}, u32[]{:S(2)}, u32[]{:S(2)}) async-start(bf16[8,536,128]{2,1,0:T(8,128)(2,1)} %get-tuple-element.11), calls=%async_computation.1 | async-start | bytes 2195456 | tf_op jit(solution)/shard_map/all_to_all | solution.py:442
  41.2 12.2 %copy-start.3 = (bf16[64,256]{1,0:T(8,128)(2,1)S(1)}, bf16[64,256]{1,0:T(8,128)(2,1)}, u32[]{:S(2)}) copy-start(bf16[64,256]{1,0:T(8,128)(2,1)} %merging.1) | copy-start | bytes 98308
  41.2 9.3 %collective-permute-start = (bf16[512,128]{1,0:T(8,128)(2,1)S(1)}, bf16[512,128]{1,0:T(8,128)(2,1)S(1)}, u32[]{:S(2)}, u32[]{:S(2)}) collective-permute-start(bf16[512,128]{1,0:T(8,128)(2,1)S(1)} %get-tuple-element.12.raw), channel_id=1, source_target_pairs={{0,1},{1,0},{2,3},{3,2},{4,5},{5,4},{6,7},{7,6},{8,9},{9,8},{10,11... | collective-permute-start | bytes 393224 | tf_op jit(solution)/shard_map/ppermute | solution.py:71
  53.4 17.5 %copy-start.1 = (bf16[256,64]{0,1:T(8,128)(2,1)S(1)}, bf16[256,64]{0,1:T(8,128)(2,1)}, u32[]{:S(2)}) copy-start(bf16[256,64]{0,1:T(8,128)(2,1)} %param.22) | copy-start | bytes 98308
  53.4 17.5 %copy-start.2 = (f32[256]{0:T(256)S(1)}, f32[256]{0:T(256)}, u32[]{:S(2)}) copy-start(f32[256]{0:T(256)} %param.21) | copy-start | bytes 3076
  70.9 50.8 %copy-start.7 = (s32[64,32]{0,1:T(8,128)S(1)}, s32[64,32]{0,1:T(8,128)}, u32[]{:S(2)}) copy-start(s32[64,32]{0,1:T(8,128)} %param.15) | copy-start | bytes 24580
  70.9 50.9 %copy-start.5 = (bf16[1024,128]{1,0:T(8,128)(2,1)S(1)}, bf16[1024,128]{1,0:T(8,128)(2,1)}, u32[]{:S(2)}) copy-start(bf16[1024,128]{1,0:T(8,128)(2,1)} %param.23) | copy-start | bytes 786436
  104.5 18.3 %copy-start = (bf16[64,32,128]{2,1,0:T(8,128)(2,1)S(1)}, bf16[64,32,128]{2,1,0:T(8,128)(2,1)}, u32[]{:S(2)}) copy-start(bf16[64,32,128]{2,1,0:T(8,128)(2,1)} %refs_4_.1) | copy-start | bytes 1572868
  104.5 11.2 %collective-permute-start.2 = (bf16[1024,128]{1,0:T(8,128)(2,1)S(1)}, bf16[1024,128]{1,0:T(8,128)(2,1)S(1)}, u32[]{:S(2)}, u32[]{:S(2)}) collective-permute-start(bf16[1024,128]{1,0:T(8,128)(2,1)S(1)} %join.1.refs_0_), channel_id=1, source_target_pairs={{0,2},{1,3},{2,0},{3,1},{4,6},{5,7},{6,4},{7,5},{8,10},{9,11},{10,... | collective-permute-start | bytes 786440 | tf_op jit(solution)/shard_map/ppermute | solution.py:71
  106.6 16.0 %collective-permute-start.1 = (bf16[1024,128]{1,0:T(8,128)(2,1)S(1)}, bf16[1024,128]{1,0:T(8,128)(2,1)S(1)}, u32[]{:S(2)}, u32[]{:S(2)}) collective-permute-start(bf16[1024,128]{1,0:T(8,128)(2,1)S(1)} %join.1.refs_0_), channel_id=1, source_target_pairs={{0,1},{1,0},{2,3},{3,2},{4,5},{5,4},{6,7},{7,6},{8,9},{9,8},{10,11... | collective-permute-start | bytes 786440 | tf_op jit(solution)/shard_map/ppermute | solution.py:71
  115.7 7.1 %collective-permute-start.3 = (bf16[1024,128]{1,0:T(8,128)(2,1)S(1)}, bf16[1024,128]{1,0:T(8,128)(2,1)S(1)}, u32[]{:S(2)}, u32[]{:S(2)}) collective-permute-start(bf16[1024,128]{1,0:T(8,128)(2,1)S(1)} %collective-permute-done.2.refs_2_), channel_id=1, source_target_pairs={{0,1},{1,0},{2,3},{3,2},{4,5},{5,4},{6,7},{7,6},{8,9},{9,8},{10,11... | collective-permute-start | bytes 786440 | tf_op jit(solution)/shard_map/ppermute | solution.py:71
